TPU v7x, 512 devices: a whole 4x4x16 slice. The times are simulated.
512 devices in a mesh: uly: 8 (over y, core), blk: 64 (over x, z).
Axes of the slice: x: 4, y: 4, z: 16, core: 2. Of those that a mesh axis runs over, the one named last changes fastest.
Arguments:
- query_inputs: bfloat16 [65536, 2048], P(('blk', 'uly')), may hold values from -6 to 6
- key_inputs: bfloat16 [65536, 1024], P(('blk', 'uly')), may hold values from -6 to 6
- value_inputs: bfloat16 [65536, 1024], P(('blk', 'uly')), may hold values from -6 to 6
- forward_out: bfloat16 [65536, 2048], P(('blk', 'uly')), may hold values from -6 to 6
- output_gradient: bfloat16 [65536, 2048], P(('blk', 'uly')), may hold values from -4 to 4
- lse_parts: float32 [65536, 16, 2], P(('blk', 'uly')), may hold values from 3 to 247
- segment_ids: int32 [65536], P(('blk', 'uly')), may hold values from 0 to 127, never falling along the last dimension, each value on 1 to 2048 neighbouring positions
Outputs:
- query_grad: bfloat16 [65536, 2048], P(('blk', 'uly'))
- key_grad: bfloat16 [65536, 1024], P(('blk', 'uly'))
- value_grad: bfloat16 [65536, 1024], P(('blk', 'uly'))
Inputs may be any that keep to these rules, and one draw needn't show every extreme that they name: `segment_ids`: never falls along the sequence; every document holds 1 to 2048 tokens, and some document exactly 2048.
All inputs are finite; a program needn't handle non-finite values.
Results may differ from a plain program's by a relative error of at most 0.0051.
Values may be sent and summed in bfloat16 or wider, within the bound.
A program may use at most 128 MiB of HBM per device.

v0:
```python
import math

import jax
import jax.numpy as jnp
from jax import lax
from jax.sharding import Mesh
from jax.sharding import PartitionSpec as P

HEAD_SIZE = 128
QUERY_HEADS = 16
KEY_VALUE_HEADS = 8
HOPS = 2
QBLOCK = 512
ULY = ("uly_0", "uly_1")
BLK_ULY = ("blk", "uly_0", "uly_1")


def cut_along(value, dim, count):
    before, after = (value.shape[:dim], value.shape[dim + 1 :])
    return jnp.moveaxis(value.reshape(*before, count, -1, *after), dim, 0)


def joined_along(pieces, dim):
    shape = list(pieces.shape[1:])
    shape[dim] *= pieces.shape[0]
    return jnp.moveaxis(pieces, 0, dim).reshape(shape)


def turned_blocks(pieces, axes, order):
    inside = pieces.shape[1:]
    whole = pieces.reshape(*(lax.axis_size(a) for a in axes), *inside)
    for k in order:
        whole = lax.all_to_all(whole, axes[k], k, k, tiled=True)
    return whole.reshape(-1, *inside)


def core_and_chips(value, groups, order, split_dim, concat_dim):
    count = lax.axis_size(groups[0]) * lax.axis_size(groups[1])
    pieces = cut_along(value, split_dim, count)
    return joined_along(turned_blocks(pieces, groups, order), concat_dim)


def sent_to_all(value, axis):
    count = lax.axis_size(axis)
    return lax.all_to_all(
        jnp.broadcast_to(value[None], (count, *value.shape)), axis, 0, 0, tiled=True
    )


def gathered_copies(value, axis, dim):
    return joined_along(sent_to_all(value, axis), dim)


def from_behind(block, axis, distance):
    devices = range(lax.axis_size(axis))
    route = [(i - distance, i) for i in devices if i - distance in devices]
    return lax.ppermute(block, axis, route)


def merge_parts(partials):
    highest = jnp.max(partials, axis=-1)
    return highest + jnp.log(jnp.sum(jnp.exp(partials - highest[..., None]), axis=-1))


def row_delta(grad_rows, out_rows):
    row_total = grad_rows.shape[0]
    products = grad_rows.astype(jnp.float32) * out_rows.astype(jnp.float32)
    return jnp.sum(products.reshape(row_total, -1, HEAD_SIZE), axis=-1)


def tile_grads(query_blk, grad_blk, lse_blk, delta_blk, key_blk, value_blk, allowed):
    score_scale = 1.0 / math.sqrt(HEAD_SIZE)
    scores = (
        jnp.einsum("mhgd,nhd->hgmn", query_blk, key_blk, preferred_element_type=jnp.float32)
        * score_scale
    )
    weights = jnp.where(allowed, jnp.exp(scores - lse_blk), 0.0)
    value_portion = jnp.einsum(
        "hgmn,mhgd->nhd", weights.astype(jnp.bfloat16), grad_blk, preferred_element_type=jnp.float32
    )
    prob_grad = jnp.einsum(
        "mhgd,nhd->hgmn", grad_blk, value_blk, preferred_element_type=jnp.float32
    )
    score_grad = (weights * (prob_grad - delta_blk)).astype(jnp.bfloat16)
    query_part = (
        jnp.einsum("hgmn,nhd->mhgd", score_grad, key_blk, preferred_element_type=jnp.float32)
        * score_scale
    )
    key_portion = (
        jnp.einsum("hgmn,mhgd->nhd", score_grad, query_blk, preferred_element_type=jnp.float32)
        * score_scale
    )
    return (query_part, key_portion, value_portion)


def per_device(
    query_inputs, key_inputs, value_inputs, forward_out, output_gradient, lse_parts, segment_ids
):
    uly_count = lax.axis_size(ULY)
    blk_place = lax.axis_index("blk")
    tok_local = query_inputs.shape[0]
    row_count = tok_local * uly_count
    group_width = QUERY_HEADS // KEY_VALUE_HEADS
    logsumexp_rows = merge_parts(lse_parts)
    row_deltas = row_delta(output_gradient, forward_out)
    query_loc, grad_loc, key_loc, value_loc = (
        core_and_chips(query_inputs, ("uly_0", "uly_1"), (1, 0), 1, 0),
        core_and_chips(output_gradient, ("uly_0", "uly_1"), (1, 0), 1, 0),
        core_and_chips(key_inputs, ("uly_0", "uly_1"), (1, 0), 1, 0),
        core_and_chips(value_inputs, ("uly_0", "uly_1"), (1, 0), 1, 0),
    )
    lse_loc, delta_loc = (
        lax.all_to_all(logsumexp_rows, ULY, split_axis=1, concat_axis=0, tiled=True),
        lax.all_to_all(row_deltas, ULY, split_axis=1, concat_axis=0, tiled=True),
    )
    ids_loc = gathered_copies(segment_ids, ULY, 0)
    kv_heads = key_loc.shape[1] // HEAD_SIZE
    query_quad = query_loc.reshape(row_count, kv_heads, group_width, HEAD_SIZE)
    gradient_quad = grad_loc.reshape(row_count, kv_heads, group_width, HEAD_SIZE)
    logsumexp_cube = lse_loc.reshape(row_count, kv_heads, group_width).transpose(1, 2, 0)[..., None]
    delta_cube = delta_loc.reshape(row_count, kv_heads, group_width).transpose(1, 2, 0)[..., None]
    key_cube = key_loc.reshape(row_count, kv_heads, HEAD_SIZE)
    value_cube = value_loc.reshape(row_count, kv_heads, HEAD_SIZE)
    rows_per_block = min(QBLOCK, row_count)
    block_total = row_count // rows_per_block
    position = jnp.arange(row_count, dtype=jnp.int32)
    query_parts = []
    key_gradient_running = jnp.zeros((row_count, kv_heads, HEAD_SIZE), jnp.float32)
    value_gradient_running = jnp.zeros((row_count, kv_heads, HEAD_SIZE), jnp.float32)
    for block_index in range(block_total):
        leading_row = block_index * rows_per_block
        finish = leading_row + rows_per_block
        allowed = (position[None, :finish] <= position[leading_row:finish, None]) & (
            ids_loc[None, :finish] == ids_loc[leading_row:finish, None]
        )
        tile_out = tile_grads(
            query_quad[leading_row:finish],
            gradient_quad[leading_row:finish],
            logsumexp_cube[:, :, leading_row:finish],
            delta_cube[:, :, leading_row:finish],
            key_cube[:finish],
            value_cube[:finish],
            allowed,
        )
        query_parts.append(tile_out[0])
        padding = ((0, row_count - finish), (0, 0), (0, 0))
        key_gradient_running = key_gradient_running + jnp.pad(tile_out[1], padding)
        value_gradient_running = value_gradient_running + jnp.pad(tile_out[2], padding)
    query_acc = jnp.concatenate(query_parts, axis=0)
    stacked_kv = jnp.stack([key_loc, value_loc])
    moved_kv = stacked_kv
    moved_ids = ids_loc
    key_parts = []
    for hop_index in range(1, HOPS + 1):
        moved_kv = from_behind(moved_kv, "blk", 1)
        moved_ids = from_behind(moved_ids, "blk", 1)
        live = (blk_place >= hop_index) & (moved_ids[-1] == ids_loc[0])
        moved_key = moved_kv[0].reshape(row_count, kv_heads, HEAD_SIZE)
        moved_value = moved_kv[1].reshape(row_count, kv_heads, HEAD_SIZE)

        def compute_tile(unused):
            query_pieces = []
            key_sum = jnp.zeros((row_count, kv_heads, HEAD_SIZE), jnp.float32)
            value_sum = jnp.zeros((row_count, kv_heads, HEAD_SIZE), jnp.float32)
            for block_index in range(block_total):
                leading_row = block_index * rows_per_block
                finish = leading_row + rows_per_block
                allowed = moved_ids[None, :] == ids_loc[leading_row:finish, None]
                tile_out = tile_grads(
                    query_quad[leading_row:finish],
                    gradient_quad[leading_row:finish],
                    logsumexp_cube[:, :, leading_row:finish],
                    delta_cube[:, :, leading_row:finish],
                    moved_key,
                    moved_value,
                    allowed,
                )
                query_pieces.append(tile_out[0])
                key_sum = key_sum + tile_out[1]
                value_sum = value_sum + tile_out[2]
            stacked = jnp.stack([key_sum.reshape(row_count, -1), value_sum.reshape(row_count, -1)])
            return (jnp.concatenate(query_pieces, axis=0), stacked)

        def skip_tile(unused):
            return (
                jnp.zeros((row_count, kv_heads, group_width, HEAD_SIZE), jnp.float32),
                jnp.zeros((2, row_count, kv_heads * HEAD_SIZE), jnp.float32),
            )

        query_more, key_more = lax.cond(live, compute_tile, skip_tile, 0)
        query_acc = query_acc + query_more
        key_parts.append(key_more)
    carried = jnp.zeros((2, row_count, kv_heads * HEAD_SIZE), jnp.float32)
    for hop_index in range(HOPS, 0, -1):
        carried = from_behind(carried + key_parts[hop_index - 1], "blk", -1)
    key_total = (key_gradient_running.reshape(row_count, -1) + carried[0]).astype(jnp.bfloat16)
    value_total = (value_gradient_running.reshape(row_count, -1) + carried[1]).astype(jnp.bfloat16)
    query_total = query_acc.reshape(row_count, -1).astype(jnp.bfloat16)
    query_grad, key_grad, value_grad = (
        lax.all_to_all(query_total, ULY, split_axis=0, concat_axis=1, tiled=True),
        lax.all_to_all(key_total, ULY, split_axis=0, concat_axis=1, tiled=True),
        lax.all_to_all(value_total, ULY, split_axis=0, concat_axis=1, tiled=True),
    )
    return (query_grad, key_grad, value_grad)


def solution(mesh):
    torus = Mesh(mesh.devices.reshape(4, 2, mesh.shape["blk"]), ("uly_0", "uly_1", "blk"))
    in_specs = (
        P(BLK_ULY, None),
        P(BLK_ULY, None),
        P(BLK_ULY, None),
        P(BLK_ULY, None),
        P(BLK_ULY, None),
        P(BLK_ULY, None, None),
        P(BLK_ULY),
    )
    out_specs = (P(BLK_ULY, None), P(BLK_ULY, None), P(BLK_ULY, None))
    return jax.shard_map(
        per_device, mesh=torus, in_specs=in_specs, out_specs=out_specs, check_vma=False
    )
```

profile of v0, /device:TPU:6, one launch (start us, length us, event | category | flops | bytes accessed | tf_op | source)
XLA Modules:
  0.0 218.4 jit_solution(10454374987237805808)
XLA Ops:
  2.7 3.6 %all-to-all-start.1 = ((bf16[4,2,128,128]{3,2,0,1:T(8,128)(2,1)}), bf16[4,2,128,128]{3,2,0,1:T(8,128)(2,1)S(1)}, u32[]{:S(2)}, u32[]{:S(2)}) async-start(bf16[4,2,128,128]{3,2,0,1:T(8,128)(2,1)} %copy.192), calls=%async_computation.1 | async-start | bytes 524288 | tf_op jit(solution)/shard_map/all_to_all | solution.py:33
  11.1 3.9 %all_to_all.123 = bf16[4,2,128,128]{3,2,0,1:T(8,128)(2,1)S(1)} all-to-all(bf16[4,2,128,128]{3,2,0,1:T(8,128)(2,1)S(1)} %copy.201), channel_id=1, replica_groups=mesh['uly_0'=4,'uly_1'=2,'blk'=64] {'uly_1'}, dimensions={1} | all-to-all | bytes 524288 | tf_op jit(solution)/shard_map/all_to_all | solution.py:33
  15.1 4.1 %all_to_all.124 = bf16[4,2,128,256]{3,2,0,1:T(8,128)(2,1)S(1)} all-to-all(bf16[4,2,128,256]{3,2,0,1:T(8,128)(2,1)S(1)} %copy.196), channel_id=1, replica_groups=mesh['uly_0'=4,'uly_1'=2,'blk'=64] {'uly_1'}, dimensions={1} | all-to-all | bytes 1048576 | tf_op jit(solution)/shard_map/all_to_all | solution.py:33
  19.2 4.1 %all_to_all.125 = bf16[4,2,128,256]{3,2,0,1:T(8,128)(2,1)S(1)} all-to-all(bf16[4,2,128,256]{3,2,0,1:T(8,128)(2,1)S(1)} %copy.205), channel_id=1, replica_groups=mesh['uly_0'=4,'uly_1'=2,'blk'=64] {'uly_1'}, dimensions={1} | all-to-all | bytes 1048576 | tf_op jit(solution)/shard_map/all_to_all | solution.py:33
  24.0 4.5 %all-to-all-start = ((s32[8,1,128]{2,1,0:T(1,128)}), s32[8,1,128]{2,1,0:T(1,128)S(1)}, u32[]{:S(2)}, u32[]{:S(2)}) async-start(s32[8,1,128]{2,1,0:T(1,128)} %broadcast_in_dim.64), calls=%async_computation | async-start | bytes 8192 | tf_op jit(solution)/shard_map/all_to_all | solution.py:45
  29.0 4.6 %all-to-all-done = s32[8,1,128]{2,1,0:T(1,128)S(1)} async-done(((s32[8,1,128]{2,1,0:T(1,128)}), s32[8,1,128]{2,1,0:T(1,128)S(1)}, u32[]{:S(2)}, u32[]{:S(2)}) %all-to-all-start) | async-done | bytes 4128 | tf_op jit(solution)/shard_map/all_to_all | solution.py:45
  49.3 3.8 %collective-permute-start = (s32[1024]{0:T(1024)S(1)}, s32[1024]{0:T(1024)S(1)}, u32[]{:S(2)}, u32[]{:S(2)}) collective-permute-start(s32[1024]{0:T(1024)S(1)} %bitcast.634), channel_id=1, source_target_pairs={{0,1},{1,2},{2,3},{3,4},{4,5},{5,6},{6,7},{7,8},{8,9},{9,10},{10,1... | collective-permute-start | bytes 12296 | tf_op jit(solution)/shard_map/ppermute | solution.py:57
  53.1 4.7 %all-to-all-start.2 = ((bf16[4,2,128,128]{3,2,1,0:T(8,128)(2,1)}), bf16[4,2,128,128]{3,2,1,0:T(8,128)(2,1)S(1)}, u32[]{:S(2)}, u32[]{:S(2)}) async-start(bf16[4,2,128,128]{3,2,1,0:T(8,128)(2,1)} %copy.193), calls=%async_computation.2 | async-start | bytes 524288 | tf_op jit(solution)/shard_map/all_to_all | solution.py:33
  57.8 6.7 %all-to-all-done.2 = bf16[4,2,128,128]{3,2,1,0:T(8,128)(2,1)S(1)} async-done(((bf16[4,2,128,128]{3,2,1,0:T(8,128)(2,1)}), bf16[4,2,128,128]{3,2,1,0:T(8,128)(2,1)S(1)}, u32[]{:S(2)}, u32[]{:S(2)}) %all-to-all-start.2) | async-done | bytes 262176 | tf_op jit(solution)/shard_map/all_to_all | solution.py:33
  69.3 5.3 %all-to-all-done.7 = bf16[4,2,128,128]{3,2,1,0:T(8,128)(2,1)S(1)} async-done(((bf16[4,2,128,128]{3,2,1,0:T(8,128)(2,1)}), bf16[4,2,128,128]{3,2,1,0:T(8,128)(2,1)S(1)}, u32[]{:S(2)}, u32[]{:S(2)}) %all-to-all-start.7) | async-done | bytes 262176 | tf_op jit(solution)/shard_map/all_to_all | solution.py:33
  74.6 3.5 %all-to-all-start.4 = ((bf16[4,2,128,256]{3,2,1,0:T(8,128)(2,1)}), bf16[4,2,128,256]{3,2,1,0:T(8,128)(2,1)S(1)}, u32[]{:S(2)}, u32[]{:S(2)}) async-start(bf16[4,2,128,256]{3,2,1,0:T(8,128)(2,1)} %copy.197), calls=%async_computation.4 | async-start | bytes 1048576 | tf_op jit(solution)/shard_map/all_to_all | solution.py:33
  79.6 3.8 %collective-permute-start.2 = (s32[1024]{0:T(1024)S(1)}, s32[1024]{0:T(1024)S(1)}, u32[]{:S(2)}, u32[]{:S(2)}) collective-permute-start(s32[1024]{0:T(1024)S(1)} %collective-permute-done), channel_id=1, source_target_pairs={{0,1},{1,2},{2,3},{3,4},{4,5},{5,6},{6,7},{7,8},{8,9},{9,10},{10,1... | collective-permute-start | bytes 12296 | tf_op jit(solution)/shard_map/ppermute | solution.py:57
  86.1 3.5 %all-to-all-start.9 = ((bf16[4,2,128,256]{3,2,1,0:T(8,128)(2,1)}), bf16[4,2,128,256]{3,2,1,0:T(8,128)(2,1)S(1)}, u32[]{:S(2)}, u32[]{:S(2)}) async-start(bf16[4,2,128,256]{3,2,1,0:T(8,128)(2,1)} %copy.206), calls=%async_computation.9 | async-start | bytes 1048576 | tf_op jit(solution)/shard_map/all_to_all | solution.py:33
  94.9 3.8 %collective-permute-start.1 = (bf16[2,1024,128]{2,1,0:T(8,128)(2,1)}, bf16[2,1024,128]{2,1,0:T(8,128)(2,1)}, u32[]{:S(2)}, u32[]{:S(2)}) collective-permute-start(bf16[2,1024,128]{2,1,0:T(8,128)(2,1)} %pad_maximum_fusion.4), channel_id=1, source_target_pairs={{0,1},{1,2},{2,3},{3,4},{4,5},{5,6},{6,7},{7,8},{8,9},{9,10},{10,1... | collective-permute-start | bytes 1572872 | tf_op jit(solution)/shard_map/ppermute | solution.py:57
  106.2 7.5 %collective-permute-done.1 = bf16[2,1024,128]{2,1,0:T(8,128)(2,1)} collective-permute-done((bf16[2,1024,128]{2,1,0:T(8,128)(2,1)}, bf16[2,1024,128]{2,1,0:T(8,128)(2,1)}, u32[]{:S(2)}, u32[]{:S(2)}) %collective-permute-start.1) | collective-permute-done | bytes 524320 | tf_op jit(solution)/shard_map/ppermute | solution.py:57
  119.7 7.8 %collective-permute-done.3 = bf16[2,1024,128]{2,1,0:T(8,128)(2,1)S(1)} collective-permute-done((bf16[2,1024,128]{2,1,0:T(8,128)(2,1)}, bf16[2,1024,128]{2,1,0:T(8,128)(2,1)S(1)}, u32[]{:S(2)}, u32[]{:S(2)}) %collective-permute-start.3) | collective-permute-done | bytes 524320 | tf_op jit(solution)/shard_map/ppermute | solution.py:57
  129.7 12.0 %collective-permute-start.4 = (f32[2,1024,128]{2,1,0:T(8,128)}, f32[2,1024,128]{2,1,0:T(8,128)}, u32[]{:S(2)}, u32[]{:S(2)}) collective-permute-start(f32[2,1024,128]{2,1,0:T(8,128)} %get-tuple-element.61), channel_id=1, source_target_pairs={{1,0},{2,1},{3,2},{4,3},{5,4},{6,5},{7,6},{8,7},{9,8},{10,9},{11,1... | collective-permute-start | bytes 3145736 | tf_op jit(solution)/shard_map/ppermute | solution.py:57
  145.5 3.9 %fusion.167 = bf16[1,2,512,1024]{2,3,1,0:T(8,128)(2,1)S(1)} fusion(f32[1024,512,2]{1,0,2:T(8,128)} %fusion.219, bf16[1024,128,1]{1,0,2:T(8,128)(2,1)} %bitcast.620, f32[2,512]{1,0:T(2,128)S(1)} %copy-done.22, f32[2,512]{1,0:T(2,128)S(1)} %copy-done.21, pred[512,1024]{0,1:T(8,128)(4,1)} %fusion.182, bf16[512,2,128]{2,1,0:T(2,128)(2,1)} %reshape.381), kind=kOutput, calls=%fused_computation.144 | convolution fusion | flops 274726912 | bytes 7348224 | tf_op jit(solution)/shard_map/mhgd,nhd->hgmn/dot_general | solution.py:81
  152.6 16.3 %conditional.2 = (f32[1024,1,2,128]{3,0,2,1:T(8,128)S(1)}, f32[2,1024,128]{2,1,0:T(8,128)S(1)}) conditional(s32[]{:T(128)} %convert_element_type.70, () %tuple.24, (s32[1024]{0:T(1024)S(1)}, s32[1024]{0:T(1024)S(1)}, bf16[2,1024,128]{2,1,0:T(8,128)(2,1)}, bf16[1024,1,2,128]{3,2,0,1:T(2,128)(2,1)S(1)}, f32[1,2,1024,1]{2,1,3,0:T(2,128)S(1)}, ...), branch_computations={%region_3.4_spmd, %region_4.5_spmd} | conditional | flops 2707554304 | bytes 55123984 | solution.py:190
  178.3 4.2 %all-to-all-start.11 = ((bf16[8,128,256]{1,2,0:T(8,128)(2,1)}), bf16[8,128,256]{1,2,0:T(8,128)(2,1)S(1)}, u32[]{:S(2)}, u32[]{:S(2)}) async-start(bf16[8,128,256]{1,2,0:T(8,128)(2,1)} %copy.218), calls=%async_computation.11 | async-start | bytes 1048576 | tf_op jit(solution)/shard_map/all_to_all | solution.py:200
  186.2 6.6 %all-to-all-done.11 = bf16[8,128,256]{1,2,0:T(8,128)(2,1)S(1)} async-done(((bf16[8,128,256]{1,2,0:T(8,128)(2,1)}), bf16[8,128,256]{1,2,0:T(8,128)(2,1)S(1)}, u32[]{:S(2)}, u32[]{:S(2)}) %all-to-all-start.11) | async-done | bytes 524320 | tf_op jit(solution)/shard_map/all_to_all | solution.py:200
  195.8 3.4 %all-to-all-start.13 = ((bf16[8,128,128]{2,1,0:T(8,128)(2,1)}), bf16[8,128,128]{2,1,0:T(8,128)(2,1)S(1)}, u32[]{:S(2)}, u32[]{:S(2)}) async-start(bf16[8,128,128]{2,1,0:T(8,128)(2,1)} %add_convert_fusion), calls=%async_computation.13 | async-start | bytes 524288 | tf_op jit(solution)/shard_map/all_to_all | solution.py:202
  200.0 6.7 %all-to-all-done.13 = bf16[8,128,128]{2,1,0:T(8,128)(2,1)S(1)} async-done(((bf16[8,128,128]{2,1,0:T(8,128)(2,1)}), bf16[8,128,128]{2,1,0:T(8,128)(2,1)S(1)}, u32[]{:S(2)}, u32[]{:S(2)}) %all-to-all-start.13) | async-done | bytes 262176 | tf_op jit(solution)/shard_map/all_to_all | solution.py:202
  210.9 6.7 %all-to-all-done.12 = bf16[8,128,128]{2,1,0:T(8,128)(2,1)S(1)} async-done(((bf16[8,128,128]{2,1,0:T(8,128)(2,1)}), bf16[8,128,128]{2,1,0:T(8,128)(2,1)S(1)}, u32[]{:S(2)}, u32[]{:S(2)}) %all-to-all-start.12) | async-done | bytes 262176 | tf_op jit(solution)/shard_map/all_to_all | solution.py:201
  (146 shorter events, 97.4 us)
Async XLA Ops:
  2.7 8.5 %all-to-all-start.1 = ((bf16[4,2,128,128]{3,2,0,1:T(8,128)(2,1)}), bf16[4,2,128,128]{3,2,0,1:T(8,128)(2,1)S(1)}, u32[]{:S(2)}, u32[]{:S(2)}) async-start(bf16[4,2,128,128]{3,2,0,1:T(8,128)(2,1)} %copy.192), calls=%async_computation.1 | async-start | bytes 524288 | tf_op jit(solution)/shard_map/all_to_all | solution.py:33
  24.0 9.7 %all-to-all-start = ((s32[8,1,128]{2,1,0:T(1,128)}), s32[8,1,128]{2,1,0:T(1,128)S(1)}, u32[]{:S(2)}, u32[]{:S(2)}) async-start(s32[8,1,128]{2,1,0:T(1,128)} %broadcast_in_dim.64), calls=%async_computation | async-start | bytes 8192 | tf_op jit(solution)/shard_map/all_to_all | solution.py:45
  33.7 34.3 %copy-start.14 = (s32[8,1,128]{2,1,0:T(1,128)}, s32[8,1,128]{2,1,0:T(1,128)S(1)}, u32[]{:S(2)}) copy-start(s32[8,1,128]{2,1,0:T(1,128)S(1)} %all-to-all-done) | copy-start | bytes 12292
  33.7 8.6 %all-to-all-start.5 = ((f32[128,8,2]{0,2,1:T(2,128)}), f32[128,8,2]{0,2,1:T(2,128)S(1)}, u32[]{:S(2)}, u32[]{:S(2)}) async-start(f32[128,8,2]{0,2,1:T(2,128)} %bitcast.95), calls=%async_computation.5 | async-start | bytes 16384 | tf_op jit(solution)/shard_map/all_to_all | solution.py:113
  42.2 10.9 %all-to-all-start.10 = ((f32[128,8,2]{0,2,1:T(2,128)}), f32[128,8,2]{0,2,1:T(2,128)S(1)}, u32[]{:S(2)}, u32[]{:S(2)}) async-start(f32[128,8,2]{0,2,1:T(2,128)} %bitcast.111), calls=%async_computation.10 | async-start | bytes 16384 | tf_op jit(solution)/shard_map/all_to_all | solution.py:114
  49.3 30.3 %collective-permute-start = (s32[1024]{0:T(1024)S(1)}, s32[1024]{0:T(1024)S(1)}, u32[]{:S(2)}, u32[]{:S(2)}) collective-permute-start(s32[1024]{0:T(1024)S(1)} %bitcast.634), channel_id=1, source_target_pairs={{0,1},{1,2},{2,3},{3,4},{4,5},{5,6},{6,7},{7,8},{8,9},{9,10},{10,1... | collective-permute-start | bytes 12296 | tf_op jit(solution)/shard_map/ppermute | solution.py:57
  53.1 11.4 %all-to-all-start.2 = ((bf16[4,2,128,128]{3,2,1,0:T(8,128)(2,1)}), bf16[4,2,128,128]{3,2,1,0:T(8,128)(2,1)S(1)}, u32[]{:S(2)}, u32[]{:S(2)}) async-start(bf16[4,2,128,128]{3,2,1,0:T(8,128)(2,1)} %copy.193), calls=%async_computation.2 | async-start | bytes 524288 | tf_op jit(solution)/shard_map/all_to_all | solution.py:33
  64.5 10.1 %all-to-all-start.7 = ((bf16[4,2,128,128]{3,2,1,0:T(8,128)(2,1)}), bf16[4,2,128,128]{3,2,1,0:T(8,128)(2,1)S(1)}, u32[]{:S(2)}, u32[]{:S(2)}) async-start(bf16[4,2,128,128]{3,2,1,0:T(8,128)(2,1)} %copy.202), calls=%async_computation.7 | async-start | bytes 524288 | tf_op jit(solution)/shard_map/all_to_all | solution.py:33
  74.6 28.8 %copy-start.10 = (bf16[4,2,128,128]{3,2,1,0:T(8,128)(2,1)}, bf16[4,2,128,128]{3,2,1,0:T(8,128)(2,1)S(1)}, u32[]{:S(2)}) copy-start(bf16[4,2,128,128]{3,2,1,0:T(8,128)(2,1)S(1)} %all-to-all-done.7) | copy-start | bytes 786436
  74.6 11.5 %all-to-all-start.4 = ((bf16[4,2,128,256]{3,2,1,0:T(8,128)(2,1)}), bf16[4,2,128,256]{3,2,1,0:T(8,128)(2,1)S(1)}, u32[]{:S(2)}, u32[]{:S(2)}) async-start(bf16[4,2,128,256]{3,2,1,0:T(8,128)(2,1)} %copy.197), calls=%async_computation.4 | async-start | bytes 1048576 | tf_op jit(solution)/shard_map/all_to_all | solution.py:33
  79.6 12.5 %collective-permute-start.2 = (s32[1024]{0:T(1024)S(1)}, s32[1024]{0:T(1024)S(1)}, u32[]{:S(2)}, u32[]{:S(2)}) collective-permute-start(s32[1024]{0:T(1024)S(1)} %collective-permute-done), channel_id=1, source_target_pairs={{0,1},{1,2},{2,3},{3,4},{4,5},{5,6},{6,7},{7,8},{8,9},{9,10},{10,1... | collective-permute-start | bytes 12296 | tf_op jit(solution)/shard_map/ppermute | solution.py:57
  86.1 14.9 %all-to-all-start.9 = ((bf16[4,2,128,256]{3,2,1,0:T(8,128)(2,1)}), bf16[4,2,128,256]{3,2,1,0:T(8,128)(2,1)S(1)}, u32[]{:S(2)}, u32[]{:S(2)}) async-start(bf16[4,2,128,256]{3,2,1,0:T(8,128)(2,1)} %copy.206), calls=%async_computation.9 | async-start | bytes 1048576 | tf_op jit(solution)/shard_map/all_to_all | solution.py:33
  94.9 18.8 %collective-permute-start.1 = (bf16[2,1024,128]{2,1,0:T(8,128)(2,1)}, bf16[2,1024,128]{2,1,0:T(8,128)(2,1)}, u32[]{:S(2)}, u32[]{:S(2)}) collective-permute-start(bf16[2,1024,128]{2,1,0:T(8,128)(2,1)} %pad_maximum_fusion.4), channel_id=1, source_target_pairs={{0,1},{1,2},{2,3},{3,4},{4,5},{5,6},{6,7},{7,8},{8,9},{9,10},{10,1... | collective-permute-start | bytes 1572872 | tf_op jit(solution)/shard_map/ppermute | solution.py:57
  106.2 21.4 %copy-start = (bf16[1024,1,2,128]{3,2,0,1:T(2,128)(2,1)S(1)}, bf16[1024,1,2,128]{3,2,0,1:T(2,128)(2,1)}, u32[]{:S(2)}) copy-start(bf16[1024,1,2,128]{3,2,0,1:T(2,128)(2,1)} %reshape_reshape_reshape.8) | copy-start | bytes 1572868
  106.2 21.4 %copy-start.2 = (bf16[1024,1,2,128]{3,2,0,1:T(2,128)(2,1)S(1)}, bf16[1024,1,2,128]{3,2,0,1:T(2,128)(2,1)}, u32[]{:S(2)}) copy-start(bf16[1024,1,2,128]{3,2,0,1:T(2,128)(2,1)} %reshape_reshape_reshape.9) | copy-start | bytes 1572868
  106.2 21.4 %copy-start.15 = (s32[8,1,128]{2,1,0:T(1,128)S(1)}, s32[8,1,128]{2,1,0:T(1,128)}, u32[]{:S(2)}) copy-start(s32[8,1,128]{2,1,0:T(1,128)} %copy-done.14) | copy-start | bytes 12292
  106.2 21.4 %copy-start.20 = (s32[1024]{0:T(1024)S(1)}, s32[1024]{0:T(1024)}, u32[]{:S(2)}) copy-start(s32[1024]{0:T(1024)} %copy-done.19) | copy-start | bytes 12292
  113.7 13.8 %collective-permute-start.3 = (bf16[2,1024,128]{2,1,0:T(8,128)(2,1)}, bf16[2,1024,128]{2,1,0:T(8,128)(2,1)S(1)}, u32[]{:S(2)}, u32[]{:S(2)}) collective-permute-start(bf16[2,1024,128]{2,1,0:T(8,128)(2,1)} %collective-permute-done.1), channel_id=1, source_target_pairs={{0,1},{1,2},{2,3},{3,4},{4,5},{5,6},{6,7},{7,8},{8,9},{9,10},{10,1... | collective-permute-start | bytes 1572872 | tf_op jit(solution)/shard_map/ppermute | solution.py:57
  129.7 39.2 %collective-permute-start.4 = (f32[2,1024,128]{2,1,0:T(8,128)}, f32[2,1024,128]{2,1,0:T(8,128)}, u32[]{:S(2)}, u32[]{:S(2)}) collective-permute-start(f32[2,1024,128]{2,1,0:T(8,128)} %get-tuple-element.61), channel_id=1, source_target_pairs={{1,0},{2,1},{3,2},{4,3},{5,4},{6,5},{7,6},{8,7},{9,8},{10,9},{11,1... | collective-permute-start | bytes 3145736 | tf_op jit(solution)/shard_map/ppermute | solution.py:57
  152.6 20.7 %copy-start.12 = (bf16[2,2,128,128]{3,2,1,0:T(8,128)(2,1)S(1)}, bf16[2,2,128,128]{3,2,1,0:T(8,128)(2,1)}, u32[]{:S(2)}) copy-start(bf16[2,2,128,128]{3,2,1,0:T(8,128)(2,1)} %slice.174) | copy-start | bytes 393220
  171.4 22.4 %collective-permute-start.5 = (f32[2,1024,128]{2,1,0:T(8,128)}, f32[2,1024,128]{2,1,0:T(8,128)}, u32[]{:S(2)}, u32[]{:S(2)}) collective-permute-start(f32[2,1024,128]{2,1,0:T(8,128)} %add.87), channel_id=1, source_target_pairs={{1,0},{2,1},{3,2},{4,3},{5,4},{6,5},{7,6},{8,7},{9,8},{10,9},{11,1... | collective-permute-start | bytes 3145736 | tf_op jit(solution)/shard_map/ppermute | solution.py:57
  178.3 14.5 %all-to-all-start.11 = ((bf16[8,128,256]{1,2,0:T(8,128)(2,1)}), bf16[8,128,256]{1,2,0:T(8,128)(2,1)S(1)}, u32[]{:S(2)}, u32[]{:S(2)}) async-start(bf16[8,128,256]{1,2,0:T(8,128)(2,1)} %copy.218), calls=%async_computation.11 | async-start | bytes 1048576 | tf_op jit(solution)/shard_map/all_to_all | solution.py:200
  195.8 10.9 %all-to-all-start.13 = ((bf16[8,128,128]{2,1,0:T(8,128)(2,1)}), bf16[8,128,128]{2,1,0:T(8,128)(2,1)S(1)}, u32[]{:S(2)}, u32[]{:S(2)}) async-start(bf16[8,128,128]{2,1,0:T(8,128)(2,1)} %add_convert_fusion), calls=%async_computation.13 | async-start | bytes 524288 | tf_op jit(solution)/shard_map/all_to_all | solution.py:202
  206.8 10.9 %all-to-all-start.12 = ((bf16[8,128,128]{2,1,0:T(8,128)(2,1)}), bf16[8,128,128]{2,1,0:T(8,128)(2,1)S(1)}, u32[]{:S(2)}, u32[]{:S(2)}) async-start(bf16[8,128,128]{2,1,0:T(8,128)(2,1)} %add_convert_fusion.1), calls=%async_computation.12 | async-start | bytes 524288 | tf_op jit(solution)/shard_map/all_to_all | solution.py:201
  (17 other events, 162.7 us)
where the time goes:
time: 221 us; the launch traced here: 218 us
  starting transfers between devices  68.1 us (31%)
  waiting for transfers between devices  57.4 us (26%)
  matrix products  34.2 us (15%)
  local copies, waits for them, and re-layouts  29.3 us (13%)
  other arithmetic  12.9 us (6%)
  blocking collectives  12.2 us (6%)
  between operations  3.88 us (2%)
    ppermute x6, starting transfers between devices, from_behind(): return lax.ppermute(block, axis, route)  27.2 us
    all_to_all x5, starting transfers between devices, turned_blocks(): whole = lax.all_to_all(whole, axes[k], k, k, tiled=True)  18.6 us
    ppermute x6, waiting for transfers between devices, from_behind(): return lax.ppermute(block, axis, route)  15.3 us
    all_to_all x5, waiting for transfers between devices, turned_blocks(): whole = lax.all_to_all(whole, axes[k], k, k, tiled=True)  14.6 us
    all_to_all x3, blocking collectives, turned_blocks(): whole = lax.all_to_all(whole, axes[k], k, k, tiled=True)  12.2 us
    dot_general x4, matrix products, tile_grads(): jnp.einsum('mhgd,nhd->hgmn', grad_blk, value_blk, preferred_element_type=...  10.1 us
    dot_general x4, matrix products, tile_grads(): jnp.einsum('mhgd,nhd->hgmn', query_blk, key_blk, preferred_element_type=j...  7.83 us
    all_to_all x1, waiting for transfers between devices, per_device(): lax.all_to_all(value_total, ULY, split_axis=0, concat_axis=1, tiled=True)  6.74 us
  transfers between devices with their start and end apart: 17, of which 10 were waited for; matrix products, arithmetic and copies ran while one was open for 30% of the time, Pallas kernels for 0%

commit v1 on v0

v1 whole, which is shorter than its diff:
```python
import math

import jax
import jax.numpy as jnp
from jax import lax
from jax.experimental import pallas as pl
from jax.experimental.pallas import tpu as pltpu
from jax.sharding import PartitionSpec as P

D = 128
HEADS = 16
GROUPS = 8
TOK = 128
ROWS = TOK * GROUPS
CH = 256
NCH = ROWS // CH
QB = 512
LOG2E = math.log2(math.e)
SCALE = 1.0 / math.sqrt(D)
MESH = pl.DeviceIdType.MESH
F32 = jnp.float32
BF16 = jnp.bfloat16


def mo(value, unit):
    return pl.multiple_of(value, unit)


def kernel(
    q_in, k_in, v_in, o_in, g_in, lp_in, id_in,
    q_out, k_out, v_out,
    Q, G, KV, ST, IDT, IDR, IDC,
    o_s, g_s, st_src, id_src,
    DQ, ACC0, ACC1, ACC2,
    S2, R2, S1, R1, SO, SQ,
    in_send, in_recv, st_send, st_recv, id_send, id_recv,
    hop_send, hop_recv, ret_send, ret_recv,
    oq_send, oq_recv, okv_send, okv_recv, loc,
):
    me = lax.axis_index("uly")
    blk = lax.axis_index("blk")
    nblk = lax.axis_size("blk")
    nxt = lax.rem(blk + 1, nblk)
    prv = lax.rem(blk + nblk - 1, nblk)

    def peer(d):
        return lax.rem(me + d, GROUPS)

    def rcopy(src, dst, ss, rs, p, b):
        return pltpu.make_async_remote_copy(
            src_ref=src, dst_ref=dst, send_sem=ss, recv_sem=rs,
            device_id=(p, b), device_id_type=MESH,
        )

    cp_g = pltpu.make_async_copy(g_in, g_s, loc.at[0])
    cp_o = pltpu.make_async_copy(o_in, o_s, loc.at[1])
    cp_g.start()
    cp_o.start()
    idrow = id_in[...].astype(F32)
    id_src[...] = jnp.broadcast_to(idrow, (8, TOK))

    barrier = pltpu.get_barrier_semaphore()

    def greet(d, _):
        pl.semaphore_signal(barrier, inc=1, device_id=(peer(d), blk), device_id_type=MESH)
        return 0

    lax.fori_loop(1, GROUPS, greet, 0)
    pl.semaphore_signal(barrier, inc=1, device_id=(me, nxt), device_id_type=MESH)
    pl.semaphore_signal(barrier, inc=1, device_id=(me, prv), device_id_type=MESH)
    pl.semaphore_wait(barrier, GROUPS + 1)

    myrow = pl.ds(mo(me * TOK, TOK), TOK)

    def in_copy(kind, p, src_i):
        row = pl.ds(mo(src_i * TOK, TOK), TOK)
        if kind == 0:
            src, dst = k_in.at[:, pl.ds(mo(p * D, D), D)], KV.at[0, row, 0:D]
        elif kind == 1:
            src, dst = v_in.at[:, pl.ds(mo(p * D, D), D)], KV.at[0, row, D : 2 * D]
        elif kind == 2:
            src, dst = q_in.at[:, pl.ds(mo(p * 2 * D, D), 2 * D)], Q.at[row, :]
        else:
            src, dst = g_in.at[:, pl.ds(mo(p * 2 * D, D), 2 * D)], G.at[row, :]
        return src, dst

    def id_copy(p, src_i):
        return rcopy(id_src, IDT.at[src_i], id_send.at[p], id_recv.at[src_i], p, blk)

    def big_copy(kind, p, src_i):
        src, dst = in_copy(kind, p, src_i)
        return rcopy(src, dst, in_send.at[kind, p], in_recv.at[kind, src_i], p, blk)

    def st_copy(p, src_i):
        return rcopy(st_src.at[p], ST.at[src_i], st_send.at[p], st_recv.at[src_i], p, blk)

    def each_peer(f):
        def body(d, _):
            f(peer(d))
            return 0

        lax.fori_loop(1, GROUPS, body, 0)

    def send_ids_kv(p):
        id_copy(p, me).start()
        big_copy(0, p, me).start()
        big_copy(1, p, me).start()

    def send_qg(p):
        big_copy(2, p, me).start()
        big_copy(3, p, me).start()

    each_peer(send_ids_kv)
    own = []
    for kind in range(4):
        src, dst = in_copy(kind, me, me)
        own.append(pltpu.make_async_copy(src, dst, loc.at[2 + kind]))
        own[-1].start()
    each_peer(send_qg)
    IDT[me] = id_src[...]

    a, b = lp_in[:, 0, :], lp_in[:, 1, :]
    top = jnp.maximum(a, b)
    lse = (top + jnp.log(jnp.exp(a - top) + jnp.exp(b - top))) * LOG2E
    cp_g.wait()
    cp_o.wait()
    lane = lax.broadcasted_iota(jnp.int32, (TOK, D), 1)

    def delta_step(h, acc):
        cols = pl.ds(mo(h * D, D), D)
        total = jnp.sum(g_s[:, cols].astype(F32) * o_s[:, cols].astype(F32), axis=1, keepdims=True)
        return jnp.where(lane == h, total, acc)

    deltas = lax.fori_loop(0, HEADS, delta_step, jnp.zeros((TOK, D), F32)).T
    for g in range(GROUPS):
        st_src[g] = jnp.concatenate(
            [lse[2 * g : 2 * g + 2], deltas[2 * g : 2 * g + 2], jnp.zeros((4, TOK), F32)], axis=0
        )

    each_peer(lambda p: id_copy(me, p).wait_recv())
    IDR[0] = IDT[:, 0, :]
    each_peer(lambda p: st_copy(p, me).start())
    ST[me] = st_src[me]

    def hop_copy(slot, c):
        rows = pl.ds(mo(c * CH, CH), CH)
        return rcopy(
            KV.at[slot, rows, :], KV.at[slot + 1, rows, :],
            hop_send.at[slot, c], hop_recv.at[slot, c], me, nxt,
        )

    def ids_hop(slot):
        return rcopy(
            IDR.at[slot], IDR.at[slot + 1], hop_send.at[slot, NCH], hop_recv.at[slot, NCH], me, nxt
        )

    def columns_of(slot):
        for s in range(GROUPS):
            tile = jnp.broadcast_to(IDR[slot, s : s + 1, :], (TOK, TOK))
            IDC[slot, s * TOK : (s + 1) * TOK, :] = tile.T

    def wait_kv(p):
        big_copy(0, me, p).wait_recv()
        big_copy(1, me, p).wait_recv()

    each_peer(wait_kv)
    own[0].wait()
    own[1].wait()
    ids_hop(0).start()
    for c in range(NCH):
        hop_copy(0, c).start()
    columns_of(0)
    ids_hop(0).wait_recv()
    ids_hop(1).start()
    columns_of(1)
    for c in range(NCH):
        hop_copy(0, c).wait_recv()
        hop_copy(1, c).start()

    def wait_qg(p):
        big_copy(2, me, p).wait_recv()
        big_copy(3, me, p).wait_recv()
        st_copy(me, p).wait_recv()

    each_peer(wait_qg)
    own[2].wait()
    own[3].wait()

    def tile(slot, c, qb, acc, causal):
        krows = pl.ds(mo(c * CH, CH), CH)
        qrows = pl.ds(mo(qb * QB, QB), QB)
        kt = KV[slot, krows, 0:D]
        vt = KV[slot, krows, D : 2 * D]
        idk = IDC[slot, krows, :]
        nq = QB // TOK
        first = qb * nq

        def row(r):
            return jnp.concatenate([ST[first + i, r : r + 1, :] for i in range(nq)], axis=1)

        idq = jnp.concatenate([IDR[0, pl.ds(first + i, 1), :] for i in range(nq)], axis=1)
        allowed = jnp.concatenate([idk] * nq, axis=1) == idq
        if causal:
            kpos = lax.broadcasted_iota(jnp.int32, (CH, QB), 0) + c * CH
            qpos = lax.broadcasted_iota(jnp.int32, (CH, QB), 1) + qb * QB
            allowed = allowed & (kpos <= qpos)
        dk = jnp.zeros((CH, D), F32)
        dv = jnp.zeros((CH, D), F32)
        for h in range(2):
            cols = slice(h * D, (h + 1) * D)
            qt = Q[qrows, cols]
            gt = G[qrows, cols]
            s = lax.dot_general(kt, qt, (((1,), (1,)), ((), ())), preferred_element_type=F32)
            w = jnp.where(allowed, jnp.exp2(s * (SCALE * LOG2E) - row(h)), 0.0)
            dp = lax.dot_general(vt, gt, (((1,), (1,)), ((), ())), preferred_element_type=F32)
            sg = (w * (dp - row(2 + h))).astype(BF16)
            dv = dv + jnp.dot(w.astype(BF16), gt, preferred_element_type=F32)
            dk = dk + jnp.dot(sg, qt, preferred_element_type=F32)
            DQ[qrows, cols] += lax.dot_general(
                sg, kt, (((0,), (0,)), ((), ())), preferred_element_type=F32
            )
        acc[krows, 0:D] += dk
        acc[krows, D : 2 * D] += dv

    DQ[...] = jnp.zeros_like(DQ)
    ACC0[...] = jnp.zeros_like(ACC0)
    ACC1[...] = jnp.zeros_like(ACC1)
    ACC2[...] = jnp.zeros_like(ACC2)

    def own_chunk(c, _):
        lax.fori_loop((c * CH) // QB, ROWS // QB, lambda qb, _: (tile(0, c, qb, ACC0, True), 0)[1], 0)
        return 0

    lax.fori_loop(0, NCH, own_chunk, 0)
    ids_hop(1).wait_recv()
    columns_of(2)

    def ret_copy(stage, c):
        rows = pl.ds(mo(c * CH, CH), CH)
        src, dst = (S2, R2) if stage == 0 else (S1, R1)
        return rcopy(
            src.at[rows, :], dst.at[rows, :], ret_send.at[stage, c], ret_recv.at[stage, c], me, prv
        )

    def pass_on(c):
        rows = pl.ds(mo(c * CH, CH), CH)
        ret_copy(0, c).wait_recv()
        S1[rows, :] = (ACC1[rows, :] + R2[rows, :].astype(F32)).astype(BF16)
        ret_copy(1, c).start()

    scales = jnp.where(lax.broadcasted_iota(jnp.int32, (CH, 2 * D), 1) < D, SCALE, 1.0)

    def hop_chunk(c, _):
        rows = pl.ds(mo(c * CH, CH), CH)
        hop_copy(1, c).wait_recv()
        trips = (c * CH) // QB + 1
        lax.fori_loop(0, trips, lambda qb, _: (tile(2, c, qb, ACC2, False), 0)[1], 0)
        S2[rows, :] = (ACC2[rows, :] * scales).astype(BF16)
        ret_copy(0, c).start()
        lax.fori_loop(0, ROWS // QB, lambda qb, _: (tile(1, c, qb, ACC1, False), 0)[1], 0)
        ACC1[rows, :] = ACC1[rows, :] * scales

        @pl.when(c > 0)
        def _():
            pass_on(c - 1)

        return 0

    lax.fori_loop(0, NCH, hop_chunk, 0)

    def oq_copy(p, src_i):
        return rcopy(
            SQ.at[pl.ds(mo(p * TOK, TOK), TOK), :],
            q_out.at[:, pl.ds(mo(src_i * 2 * D, D), 2 * D)],
            oq_send.at[p], oq_recv.at[src_i], p, blk,
        )

    SQ[...] = (DQ[...] * SCALE).astype(BF16)
    each_peer(lambda p: oq_copy(p, me).start())
    own_q = pltpu.make_async_copy(
        SQ.at[myrow, :], q_out.at[:, pl.ds(mo(me * 2 * D, D), 2 * D)], loc.at[6]
    )
    own_q.start()
    pass_on(NCH - 1)

    def okv_copy(kind, p, src_i):
        src = SO.at[pl.ds(mo(p * TOK, TOK), TOK), kind * D : (kind + 1) * D]
        dst = (k_out, v_out)[kind].at[:, pl.ds(mo(src_i * D, D), D)]
        return rcopy(src, dst, okv_send.at[kind, p], okv_recv.at[kind, src_i], p, blk)

    def own_kv(kind):
        src = SO.at[myrow, kind * D : (kind + 1) * D]
        dst = (k_out, v_out)[kind].at[:, pl.ds(mo(me * D, D), D)]
        return pltpu.make_async_copy(src, dst, loc.at[7 + kind])

    per = CH // TOK

    def out_chunk(c, _):
        rows = pl.ds(mo(c * CH, CH), CH)
        ret_copy(1, c).wait_recv()
        SO[rows, :] = (ACC0[rows, :] * scales + R1[rows, :].astype(F32)).astype(BF16)
        for i in range(per):
            p = c * per + i

            @pl.when(p != me)
            def _():
                okv_copy(0, p, me).start()
                okv_copy(1, p, me).start()

            @pl.when(p == me)
            def _():
                own_kv(0).start()
                own_kv(1).start()

        return 0

    lax.fori_loop(0, NCH, out_chunk, 0)

    def drain_sends(p):
        id_copy(p, me).wait_send()
        for kind in range(4):
            big_copy(kind, p, me).wait_send()
        st_copy(p, me).wait_send()
        oq_copy(p, me).wait_send()
        okv_copy(0, p, me).wait_send()
        okv_copy(1, p, me).wait_send()

    each_peer(drain_sends)
    for slot in range(2):
        ids_hop(slot).wait_send()
    for stage in range(2):
        for c in range(NCH):
            hop_copy(stage, c).wait_send()
            ret_copy(stage, c).wait_send()

    def drain_recvs(p):
        oq_copy(me, p).wait_recv()
        okv_copy(0, me, p).wait_recv()
        okv_copy(1, me, p).wait_recv()

    each_peer(drain_recvs)
    own_q.wait()
    own_kv(0).wait()
    own_kv(1).wait()


def per_device(q, k, v, o, g, lp, ids):
    lp = lp.transpose(1, 2, 0)
    ids = ids.reshape(1, TOK)
    any_spec = pl.BlockSpec(memory_space=pl.ANY)
    vmem = pl.BlockSpec(memory_space=pltpu.VMEM)
    dma = pltpu.SemaphoreType.DMA
    scratch = [
        pltpu.VMEM((ROWS, 2 * D), BF16),
        pltpu.VMEM((ROWS, 2 * D), BF16),
        pltpu.VMEM((3, ROWS, 2 * D), BF16),
        pltpu.VMEM((GROUPS, 8, TOK), F32),
        pltpu.VMEM((GROUPS, 8, TOK), F32),
        pltpu.VMEM((3, GROUPS, TOK), F32),
        pltpu.VMEM((3, ROWS, TOK), F32),
        pltpu.VMEM((TOK, HEADS * D), BF16),
        pltpu.VMEM((TOK, HEADS * D), BF16),
        pltpu.VMEM((GROUPS, 8, TOK), F32),
        pltpu.VMEM((8, TOK), F32),
        pltpu.VMEM((ROWS, 2 * D), F32),
        pltpu.VMEM((ROWS, 2 * D), F32),
        pltpu.VMEM((ROWS, 2 * D), F32),
        pltpu.VMEM((ROWS, 2 * D), F32),
        pltpu.VMEM((ROWS, 2 * D), BF16),
        pltpu.VMEM((ROWS, 2 * D), BF16),
        pltpu.VMEM((ROWS, 2 * D), BF16),
        pltpu.VMEM((ROWS, 2 * D), BF16),
        pltpu.VMEM((ROWS, 2 * D), BF16),
        pltpu.VMEM((ROWS, 2 * D), BF16),
        dma((4, GROUPS)), dma((4, GROUPS)),
        dma((GROUPS,)), dma((GROUPS,)),
        dma((GROUPS,)), dma((GROUPS,)),
        dma((2, NCH + 1)), dma((2, NCH + 1)),
        dma((2, NCH)), dma((2, NCH)),
        dma((GROUPS,)), dma((GROUPS,)),
        dma((2, GROUPS)), dma((2, GROUPS)),
        dma((9,)),
    ]
    return pl.pallas_call(
        kernel,
        out_shape=(
            jax.ShapeDtypeStruct((TOK, HEADS * D), BF16),
            jax.ShapeDtypeStruct((TOK, GROUPS * D), BF16),
            jax.ShapeDtypeStruct((TOK, GROUPS * D), BF16),
        ),
        in_specs=[any_spec] * 5 + [vmem, vmem],
        out_specs=(any_spec,) * 3,
        scratch_shapes=scratch,
        compiler_params=pltpu.CompilerParams(
            collective_id=0, has_side_effects=True, vmem_limit_bytes=48 * 1024 * 1024
        ),
        name="attention_backward",
    )(q, k, v, o, g, lp, ids)


def solution(mesh):
    tokens = ("blk", "uly")
    row = P(tokens, None)
    in_specs = (row, row, row, row, row, P(tokens, None, None), P(tokens))
    return jax.shard_map(
        per_device, mesh=mesh, in_specs=in_specs, out_specs=(row, row, row), check_vma=False
    )
```

time: 221 us -> 85.3 us (0.39)
  the two profiles are of different devices: /device:TPU:6 before, /device:TPU:1 now
where the time goes in v1:
time: 85.3 us; the launch traced here: 84.9 us
  Pallas kernels  75.7 us (89%)
  local copies, waits for them, and re-layouts  8.59 us (10%)
    pallas_call x1, Pallas kernels, per_device(): pl.pallas_call(kernel, out_shape=(jax.ShapeDtypeStruct((TOK, HEADS * D),...  75.7 us
    unnamed x17, local copies, waits for them, and re-layouts  8.59 us

profile of v1, /device:TPU:1, one launch (start us, length us, event | category | flops | bytes accessed | tf_op | source)
XLA Modules:
  0.0 84.9 jit_solution(2792732537106535780)
XLA Ops:
  0.6 0.0 copy-start.6
  0.6 0.6 copy-done.6
  1.3 0.0 copy-start
  1.3 1.0 %copy-done = bf16[128,2048]{1,0:T(8,128)(2,1)S(1)} copy-done((bf16[128,2048]{1,0:T(8,128)(2,1)S(1)}, bf16[128,2048]{1,0:T(8,128)(2,1)}, u32[]{:S(2)}) %copy-start) | copy-done | bytes 524312
  2.3 0.0 copy-start.1
  2.3 1.0 %copy-done.1 = bf16[128,2048]{1,0:T(8,128)(2,1)S(1)} copy-done((bf16[128,2048]{1,0:T(8,128)(2,1)S(1)}, bf16[128,2048]{1,0:T(8,128)(2,1)}, u32[]{:S(2)}) %copy-start.1) | copy-done | bytes 524312
  3.4 0.0 copy-start.2
  3.4 1.0 %copy-done.2 = bf16[128,2048]{1,0:T(8,128)(2,1)S(1)} copy-done((bf16[128,2048]{1,0:T(8,128)(2,1)S(1)}, bf16[128,2048]{1,0:T(8,128)(2,1)}, u32[]{:S(2)}) %copy-start.2) | copy-done | bytes 524312
  4.4 0.0 copy-start.3
  4.4 0.9 %copy-done.3 = bf16[128,1024]{1,0:T(8,128)(2,1)S(1)} copy-done((bf16[128,1024]{1,0:T(8,128)(2,1)S(1)}, bf16[128,1024]{1,0:T(8,128)(2,1)}, u32[]{:S(2)}) %copy-start.3) | copy-done | bytes 262168
  5.4 0.0 copy-start.4
  5.4 0.9 %copy-done.4 = bf16[128,1024]{1,0:T(8,128)(2,1)S(1)} copy-done((bf16[128,1024]{1,0:T(8,128)(2,1)S(1)}, bf16[128,1024]{1,0:T(8,128)(2,1)}, u32[]{:S(2)}) %copy-start.4) | copy-done | bytes 262168
  6.3 0.0 copy-start.5
  6.3 0.7 copy-done.5
  7.0 75.7 %attention_backward.1 = (bf16[128,2048]{1,0:T(8,128)(2,1)S(1)}, bf16[128,1024]{1,0:T(8,128)(2,1)S(1)}, bf16[128,1024]{1,0:T(8,128)(2,1)S(1)}) custom-call(bf16[128,2048]{1,0:T(8,128)(2,1)S(1)} %copy-done, bf16[128,1024]{1,0:T(8,128)(2,1)S(1)} %copy-done.3, bf16[128,1024]{1,0:T(8,128)(2,1)S(1)} %copy-done.4, bf16[128,2048]{1,0:T(8,128)(2,1)S(1)} %copy-done.1, ...), custom_call_target="tpu_custom_call" | custom-call | tf_op jit(solution)/shard_map/attention_backward/pallas_call | solution.py:384
  82.7 0.8 copy.13
  83.5 0.7 copy.14
  84.2 0.7 copy.15
Async XLA Ops:
  0.6 0.7 copy-start.6
  1.3 1.0 %copy-start = (bf16[128,2048]{1,0:T(8,128)(2,1)S(1)}, bf16[128,2048]{1,0:T(8,128)(2,1)}, u32[]{:S(2)}) copy-start(bf16[128,2048]{1,0:T(8,128)(2,1)} %q_in.1) | copy-start | bytes 1572868
  2.3 1.0 %copy-start.1 = (bf16[128,2048]{1,0:T(8,128)(2,1)S(1)}, bf16[128,2048]{1,0:T(8,128)(2,1)}, u32[]{:S(2)}) copy-start(bf16[128,2048]{1,0:T(8,128)(2,1)} %o_in.1) | copy-start | bytes 1572868
  3.4 1.0 %copy-start.2 = (bf16[128,2048]{1,0:T(8,128)(2,1)S(1)}, bf16[128,2048]{1,0:T(8,128)(2,1)}, u32[]{:S(2)}) copy-start(bf16[128,2048]{1,0:T(8,128)(2,1)} %g_in.1) | copy-start | bytes 1572868
  4.4 0.9 %copy-start.3 = (bf16[128,1024]{1,0:T(8,128)(2,1)S(1)}, bf16[128,1024]{1,0:T(8,128)(2,1)}, u32[]{:S(2)}) copy-start(bf16[128,1024]{1,0:T(8,128)(2,1)} %k_in.1) | copy-start | bytes 786436
  5.4 0.9 %copy-start.4 = (bf16[128,1024]{1,0:T(8,128)(2,1)S(1)}, bf16[128,1024]{1,0:T(8,128)(2,1)}, u32[]{:S(2)}) copy-start(bf16[128,1024]{1,0:T(8,128)(2,1)} %v_in.1) | copy-start | bytes 786436
  6.3 0.7 copy-start.5

commit v2 on v1

v2 whole, which is shorter than its diff:
```python
import math

import jax
import jax.numpy as jnp
from jax import lax
from jax.experimental import pallas as pl
from jax.experimental.pallas import tpu as pltpu
from jax.sharding import PartitionSpec as P

D = 128
HEADS = 16
GROUPS = 8
TOK = 128
ROWS = TOK * GROUPS
CH = 256
NCH = ROWS // CH
NY = 4
QB = 512
LOG2E = math.log2(math.e)
SCALE = 1.0 / math.sqrt(D)
MESH = pl.DeviceIdType.MESH
F32 = jnp.float32
BF16 = jnp.bfloat16


def mo(value, unit):
    return pl.multiple_of(value, unit)


def kernel(
    q_in, k_in, v_in, o_in, g_in, lp_in, id_in,
    q_out, k_out, v_out,
    Q, G, KV, ST, IDT, IDR, IDC,
    o_s, g_s, q_s, st_src, id_src, SKV, PKV, PQ, PG,
    DQ, ACC0, ACC1, ACC2,
    S2, R2, S1, R1, SO, SQ, XQ, XKV,
    loc, skv_sem, d2d_send, d2d_recv, yo_send, yo_recv,
    st_send, st_recv, id_send, id_recv,
    hop_send, hop_recv, ret_send, ret_recv,
    oq_send, oq_recv, okv_send, okv_recv, fwd_send, fwd_recv, lout,
):
    me = lax.axis_index("uly")
    blk = lax.axis_index("blk")
    nblk = lax.axis_size("blk")
    nxt = lax.rem(blk + 1, nblk)
    prv = lax.rem(blk + nblk - 1, nblk)
    y = me // 2
    core = lax.rem(me, 2)
    mate = me + 1 - 2 * core

    def rcopy(src, dst, ss, rs, p, b):
        return pltpu.make_async_remote_copy(
            src_ref=src, dst_ref=dst, send_sem=ss, recv_sem=rs,
            device_id=(p, b), device_id_type=MESH,
        )

    def peer(d):
        return lax.rem(me + d, GROUPS)

    def each_peer(f):
        def body(d, _):
            f(peer(d))
            return 0

        lax.fori_loop(1, GROUPS, body, 0)

    pair = y // 2

    def chip(k):
        step = k + (k // 2) * (5 - 2 * k)
        return lax.rem(y + (1 - 2 * lax.rem(y, 2)) * step + NY, NY)

    def rows_of(u):
        return pl.ds(mo(u * TOK, TOK), TOK)

    def chunk(c):
        return pl.ds(mo(c * CH, CH), CH)

    def wide(g):
        return pl.ds(mo(g * 2 * D, 2 * D), 2 * D)

    def narrow(g):
        return pl.ds(mo(g * D, D), D)

    cp_g = pltpu.make_async_copy(g_in, g_s, loc.at[0])
    cp_o = pltpu.make_async_copy(o_in, o_s, loc.at[1])
    cp_q = pltpu.make_async_copy(q_in, q_s, loc.at[6])

    def stage_kv(g):
        return (
            pltpu.make_async_copy(k_in.at[:, narrow(g)], SKV.at[g, :, 0:D], skv_sem.at[0, g]),
            pltpu.make_async_copy(v_in.at[:, narrow(g)], SKV.at[g, :, D : 2 * D], skv_sem.at[1, g]),
        )

    own = [
        pltpu.make_async_copy(k_in.at[:, narrow(me)], KV.at[0, rows_of(me), 0:D], loc.at[2]),
        pltpu.make_async_copy(v_in.at[:, narrow(me)], KV.at[0, rows_of(me), D : 2 * D], loc.at[3]),
        pltpu.make_async_copy(q_in.at[:, wide(me)], Q.at[rows_of(me), :], loc.at[4]),
        pltpu.make_async_copy(g_in.at[:, wide(me)], G.at[rows_of(me), :], loc.at[5]),
    ]

    barrier = pltpu.get_barrier_semaphore()

    def greet(d, _):
        pl.semaphore_signal(barrier, inc=1, device_id=(peer(d), blk), device_id_type=MESH)
        return 0

    lax.fori_loop(1, GROUPS, greet, 0)
    pl.semaphore_signal(barrier, inc=1, device_id=(me, nxt), device_id_type=MESH)
    pl.semaphore_signal(barrier, inc=1, device_id=(me, prv), device_id_type=MESH)

    def stage_step(g, _):
        for cp in stage_kv(g):
            cp.start()
        return 0

    lax.fori_loop(0, GROUPS, stage_step, 0)
    for cp in own:
        cp.start()
    cp_q.start()
    cp_g.start()
    cp_o.start()
    id_src[...] = jnp.broadcast_to(id_in[...].astype(F32), (8, TOK))

    def stage_wait(g, _):
        for cp in stage_kv(g):
            cp.wait()
        return 0

    lax.fori_loop(0, GROUPS, stage_wait, 0)
    pl.semaphore_wait(barrier, GROUPS + 1)

    def mate_copy(kind, t, here, there, same):
        g = 2 * t + lax.rem(there, 2)
        src = (SKV.at[g], q_s.at[:, wide(g)], g_s.at[:, wide(g)])[kind]
        if same:
            dst = (KV.at[0, rows_of(here), :], Q.at[rows_of(here), :], G.at[rows_of(here), :])[kind]
        else:
            dst = (PKV, PQ, PG)[kind].at[t]
        return rcopy(src, dst, d2d_send.at[kind, t], d2d_recv.at[kind, t], mate, blk)

    def mate_send(kind, k):
        return mate_copy(kind, chip(k), me, mate, k == 0)

    def mate_recv(kind, k):
        return mate_copy(kind, chip(k), mate, me, k == 0)

    for k in range(NY):
        mate_send(0, k).start()

    def id_copy(p, src_i):
        return rcopy(id_src, IDT.at[src_i], id_send.at[p], id_recv.at[src_i], p, blk)

    def st_copy(p, src_i):
        return rcopy(st_src.at[p], ST.at[src_i], st_send.at[p], st_recv.at[src_i], p, blk)

    each_peer(lambda p: id_copy(p, me).start())

    def y_copy(kind, part, t, s):
        g = 2 * t + core
        u = 2 * s + (core if part == 0 else 1 - core)
        if part == 0:
            src = (SKV.at[g], q_s.at[:, wide(g)], g_s.at[:, wide(g)])[kind]
        else:
            src = (PKV, PQ, PG)[kind].at[t]
        dst = (KV.at[0, rows_of(u), :], Q.at[rows_of(u), :], G.at[rows_of(u), :])[kind]
        return rcopy(
            src, dst, yo_send.at[kind, part, t], yo_recv.at[kind, part, s], g, blk
        )

    def hop_copy(slot, c):
        rows = chunk(c)
        return rcopy(
            KV.at[slot, rows, :], KV.at[slot + 1, rows, :],
            hop_send.at[slot, c], hop_recv.at[slot, c], me, nxt,
        )

    def ids_hop(slot):
        return rcopy(
            IDR.at[slot], IDR.at[slot + 1], hop_send.at[slot, NCH], hop_recv.at[slot, NCH], me, nxt
        )

    for k in range(1, NY):
        y_copy(0, 0, chip(k), y).start()
    cp_q.wait()
    cp_g.wait()
    for kind in (1, 2):
        for k in range(NY):
            mate_send(kind, k).start()
    own[0].wait()
    own[1].wait()
    mate_recv(0, 0).wait_recv()
    hop_copy(0, chip(0)).start()
    for k in range(1, NY):
        mate_recv(0, k).wait_recv()
        y_copy(0, 1, chip(k), y).start()
    for near in ((1, 2), (3,)):
        for k in near:
            for kind in (1, 2):
                y_copy(kind, 0, chip(k), y).start()
        for k in near:
            for kind in (1, 2):
                mate_recv(kind, k).wait_recv()
                y_copy(kind, 1, chip(k), y).start()

    IDT[me] = id_src[...]
    each_peer(lambda p: id_copy(me, p).wait_recv())
    IDR[0] = IDT[:, 0, :]

    def columns_of(slot):
        for s in range(GROUPS):
            tile = jnp.broadcast_to(IDR[slot, s : s + 1, :], (TOK, TOK))
            IDC[slot, s * TOK : (s + 1) * TOK, :] = tile.T

    def wait_kv(k):
        y_copy(0, 0, y, chip(k)).wait_recv()
        y_copy(0, 1, y, chip(k)).wait_recv()

    wait_kv(1)
    ids_hop(0).start()
    hop_copy(0, chip(1)).start()

    a, b = lp_in[:, 0, :], lp_in[:, 1, :]
    top = jnp.maximum(a, b)
    lse = (top + jnp.log(jnp.exp(a - top) + jnp.exp(b - top))) * LOG2E
    cp_o.wait()
    lane = lax.broadcasted_iota(jnp.int32, (TOK, D), 1)

    def delta_step(h, acc):
        cols = narrow(h)
        total = jnp.sum(g_s[:, cols].astype(F32) * o_s[:, cols].astype(F32), axis=1, keepdims=True)
        return jnp.where(lane == h, total, acc)

    deltas = lax.fori_loop(0, HEADS, delta_step, jnp.zeros((TOK, D), F32)).T
    for g in range(GROUPS):
        st_src[g] = jnp.concatenate(
            [lse[2 * g : 2 * g + 2], deltas[2 * g : 2 * g + 2], jnp.zeros((4, TOK), F32)], axis=0
        )
    ST[me] = st_src[me]
    each_peer(lambda p: st_copy(p, me).start())

    hop_copy(0, chip(0)).wait_recv()
    hop_copy(1, chip(0)).start()
    wait_kv(2)
    hop_copy(0, chip(2)).start()
    ids_hop(0).wait_recv()
    ids_hop(1).start()
    hop_copy(0, chip(1)).wait_recv()
    hop_copy(1, chip(1)).start()
    wait_kv(3)
    hop_copy(0, chip(3)).start()

    columns_of(0)
    columns_of(1)
    DQ[...] = jnp.zeros_like(DQ)
    ACC0[...] = jnp.zeros_like(ACC0)
    ACC1[...] = jnp.zeros_like(ACC1)
    ACC2[...] = jnp.zeros_like(ACC2)

    def tile(slot, c, qb, acc, causal, depth):
        krows = pl.ds(mo(c * depth, depth), depth)
        qrows = pl.ds(mo(qb * QB, QB), QB)
        kt = KV[slot, krows, 0:D]
        vt = KV[slot, krows, D : 2 * D]
        idk = IDC[slot, krows, :]
        nq = QB // TOK
        first = qb * nq

        def row(r):
            return jnp.concatenate([ST[first + i, r : r + 1, :] for i in range(nq)], axis=1)

        idq = jnp.concatenate([IDR[0, pl.ds(first + i, 1), :] for i in range(nq)], axis=1)
        allowed = jnp.concatenate([idk] * nq, axis=1) == idq
        if causal:
            kpos = lax.broadcasted_iota(jnp.int32, (depth, QB), 0) + c * depth
            qpos = lax.broadcasted_iota(jnp.int32, (depth, QB), 1) + qb * QB
            allowed = allowed & (kpos <= qpos)
        dk = jnp.zeros((depth, D), F32)
        dv = jnp.zeros((depth, D), F32)
        turned = kt.T
        for h in range(2):
            cols = slice(h * D, (h + 1) * D)
            qt = Q[qrows, cols]
            gt = G[qrows, cols]
            s = lax.dot_general(kt, qt, (((1,), (1,)), ((), ())), preferred_element_type=F32)
            w = jnp.where(allowed, jnp.exp2(s * (SCALE * LOG2E) - row(h)), 0.0)
            dp = lax.dot_general(vt, gt, (((1,), (1,)), ((), ())), preferred_element_type=F32)
            sg = (w * (dp - row(2 + h))).astype(BF16)
            dv = dv + jnp.dot(w.astype(BF16), gt, preferred_element_type=F32)
            dk = dk + jnp.dot(sg, qt, preferred_element_type=F32)
            DQ[cols, qrows] += jnp.dot(turned, sg, preferred_element_type=F32)
        acc[krows, 0:D] += dk
        acc[krows, D : 2 * D] += dv

    def wait_qg(k):
        for kind in (1, 2):
            y_copy(kind, 0, y, chip(k)).wait_recv()
            y_copy(kind, 1, y, chip(k)).wait_recv()

    def own_tiles(qb, count):
        lax.fori_loop(0, count, lambda c, _: (tile(0, c, qb, ACC0, True, QB), 0)[1], 0)

    each_peer(lambda p: st_copy(me, p).wait_recv())
    own[2].wait()
    own[3].wait()
    mate_recv(1, 0).wait_recv()
    mate_recv(2, 0).wait_recv()
    wait_qg(1)
    own_tiles(pair, pair + 1)
    hop_copy(0, chip(2)).wait_recv()
    hop_copy(1, chip(2)).start()
    wait_qg(2)
    wait_qg(3)
    ids_hop(1).wait_recv()
    columns_of(2)

    def ret_copy(stage, c):
        rows = chunk(c)
        src, dst = (S2, R2) if stage == 0 else (S1, R1)
        return rcopy(
            src.at[rows, :], dst.at[rows, :], ret_send.at[stage, c], ret_recv.at[stage, c], me, prv
        )

    scales = jnp.where(lax.broadcasted_iota(jnp.int32, (CH, 2 * D), 1) < D, SCALE, 1.0)

    def hop_two(c):
        hop_copy(1, c).wait_recv()
        trips = (c * CH) // QB + 1
        lax.fori_loop(0, trips, lambda qb, _: (tile(2, c, qb, ACC2, False, CH), 0)[1], 0)
        S2[chunk(c), :] = (ACC2[chunk(c), :] * scales).astype(BF16)
        ret_copy(0, c).start()

    def pass_on(c):
        ret_copy(0, c).wait_recv()
        S1[chunk(c), :] = (ACC1[chunk(c), :] * scales + R2[chunk(c), :].astype(F32)).astype(BF16)
        ret_copy(1, c).start()

    def hop_one(half):
        lax.fori_loop(0, ROWS // QB, lambda qb, _: (tile(1, half, qb, ACC1, False, QB), 0)[1], 0)

    def okv_copy(t, s):
        return rcopy(
            SO.at[chunk(t), :], XKV.at[s], okv_send.at[t], okv_recv.at[s], 2 * t + core, blk
        )

    def oq_copy(t, s):
        return rcopy(
            SQ.at[chunk(t), :], XQ.at[s], oq_send.at[t], oq_recv.at[s], 2 * t + core, blk
        )

    def total(c):
        ret_copy(1, c).wait_recv()
        return (ACC0[chunk(c), :] * scales + R1[chunk(c), :].astype(F32)).astype(BF16)

    def out_chunk(k):
        c = chip(k)
        SO[chunk(c), :] = total(c)
        okv_copy(c, y).start()

    def round_trip(j, _):
        hop_two(chip(j))

        @pl.when(j == 0)
        def _():
            hop_copy(0, chip(3)).wait_recv()
            hop_copy(1, chip(3)).start()

        @pl.when(lax.rem(j, 2) == 1)
        def _():
            own_tiles(1 - pair, (2 - pair) * ((3 - j) // 2))
            hop_one(pair + (1 - 2 * pair) * (j // 2))
            pass_on(chip(j - 1))
            pass_on(chip(j))

        return 0

    lax.fori_loop(0, NCH, round_trip, 0)
    out_chunk(1)

    mine = pl.ds(mo(core * TOK, TOK), TOK)
    theirs = pl.ds(mo((1 - core) * TOK, TOK), TOK)

    def forward(s, kind, owner):
        g = 2 * s + lax.rem(owner, 2)
        if kind == 0:
            src, dst = XQ.at[s, theirs, :], q_out.at[:, wide(g)]
        elif kind == 1:
            src, dst = XKV.at[s, theirs, 0:D], k_out.at[:, narrow(g)]
        else:
            src, dst = XKV.at[s, theirs, D : 2 * D], v_out.at[:, narrow(g)]
        return rcopy(src, dst, fwd_send.at[kind, s], fwd_recv.at[kind, s], mate, blk)

    def keep(s, kind):
        g = 2 * s + core
        if kind == 0:
            src, dst = XQ.at[s, mine, :], q_out.at[:, wide(g)]
        elif kind == 1:
            src, dst = XKV.at[s, mine, 0:D], k_out.at[:, narrow(g)]
        else:
            src, dst = XKV.at[s, mine, D : 2 * D], v_out.at[:, narrow(g)]
        return pltpu.make_async_copy(src, dst, lout.at[kind, s])

    def deliver(s, kind):
        forward(s, kind, me).start()
        keep(s, kind).start()

    def turn(c):
        return (DQ[:, chunk(c)] * SCALE).T.astype(BF16)

    def send_q(k, _):
        c = chip(k)
        SQ[chunk(c), :] = turn(c)
        oq_copy(c, y).start()
        return 0

    lax.fori_loop(1, NY, send_q, 0)
    XKV[y] = total(y)
    deliver(y, 1)
    deliver(y, 2)
    XQ[y] = turn(y)
    deliver(y, 0)
    out_chunk(2)
    out_chunk(3)

    def arrivals(k, _):
        s = chip(k)
        oq_copy(y, s).wait_recv()
        deliver(s, 0)
        return 0

    lax.fori_loop(1, NY, arrivals, 0)

    def arrivals_kv(k, _):
        s = chip(k)
        okv_copy(y, s).wait_recv()
        deliver(s, 1)
        deliver(s, 2)
        return 0

    lax.fori_loop(1, NY, arrivals_kv, 0)

    def drain_small(p):
        id_copy(p, me).wait_send()
        st_copy(p, me).wait_send()

    each_peer(drain_small)
    for slot in range(2):
        ids_hop(slot).wait_send()
    for stage in range(2):
        for c in range(NCH):
            hop_copy(stage, c).wait_send()
            ret_copy(stage, c).wait_send()
    for k in range(NY):
        for kind in range(3):
            mate_send(kind, k).wait_send()
            if k > 0:
                y_copy(kind, 0, chip(k), y).wait_send()
                y_copy(kind, 1, chip(k), y).wait_send()
        if k > 0:
            oq_copy(chip(k), y).wait_send()
            okv_copy(chip(k), y).wait_send()

    def drain_out(s, _):
        for kind in range(3):
            forward(s, kind, me).wait_send()
            keep(s, kind).wait()
            forward(s, kind, mate).wait_recv()
        return 0

    lax.fori_loop(0, NY, drain_out, 0)


def publish(q_in, k_in, v_in, q_out, k_out, v_out, q_s, k_s, v_s, read, write):
    moves = ((q_in, q_s, q_out), (k_in, k_s, k_out), (v_in, v_s, v_out))
    reads = [pltpu.make_async_copy(a, b, read.at[i]) for i, (a, b, _) in enumerate(moves)]
    writes = [pltpu.make_async_copy(b, c, write.at[i]) for i, (_, b, c) in enumerate(moves)]
    for cp in reads:
        cp.start()
    for cp, back in zip(reads, writes):
        cp.wait()
        back.start()
    for cp in writes:
        cp.wait()


def per_device(q, k, v, o, g, lp, ids):
    lp = lp.transpose(1, 2, 0)
    ids = ids.reshape(1, TOK)
    any_spec = pl.BlockSpec(memory_space=pl.ANY)
    vmem = pl.BlockSpec(memory_space=pltpu.VMEM)
    dma = pltpu.SemaphoreType.DMA
    slab = pltpu.VMEM((ROWS, 2 * D), BF16)
    acc = pltpu.VMEM((ROWS, 2 * D), F32)
    block = pltpu.VMEM((NY, TOK, 2 * D), BF16)
    scratch = [
        slab,
        slab,
        pltpu.VMEM((3, ROWS, 2 * D), BF16),
        pltpu.VMEM((GROUPS, 8, TOK), F32),
        pltpu.VMEM((GROUPS, 8, TOK), F32),
        pltpu.VMEM((3, GROUPS, TOK), F32),
        pltpu.VMEM((3, ROWS, TOK), F32),
        pltpu.VMEM((TOK, HEADS * D), BF16),
        pltpu.VMEM((TOK, HEADS * D), BF16),
        pltpu.VMEM((TOK, HEADS * D), BF16),
        pltpu.VMEM((GROUPS, 8, TOK), F32),
        pltpu.VMEM((8, TOK), F32),
        pltpu.VMEM((GROUPS, TOK, 2 * D), BF16),
        block, block, block,
        pltpu.VMEM((2 * D, ROWS), F32),
        acc, acc, acc,
        slab, slab, slab, slab, slab, slab,
        pltpu.VMEM((NY, CH, 2 * D), BF16),
        pltpu.VMEM((NY, CH, 2 * D), BF16),
        dma((7,)), dma((2, GROUPS)),
        dma((3, NY)), dma((3, NY)),
        dma((3, 2, NY)), dma((3, 2, NY)),
        dma((GROUPS,)), dma((GROUPS,)),
        dma((GROUPS,)), dma((GROUPS,)),
        dma((2, NCH + 1)), dma((2, NCH + 1)),
        dma((2, NCH)), dma((2, NCH)),
        dma((NY,)), dma((NY,)), dma((NY,)), dma((NY,)),
        dma((3, NY)), dma((3, NY)), dma((3, NY)),
    ]
    shapes = (
        jax.ShapeDtypeStruct((TOK, HEADS * D), BF16),
        jax.ShapeDtypeStruct((TOK, GROUPS * D), BF16),
        jax.ShapeDtypeStruct((TOK, GROUPS * D), BF16),
    )
    grads = pl.pallas_call(
        kernel,
        out_shape=shapes,
        in_specs=[any_spec] * 5 + [vmem, vmem],
        out_specs=(any_spec,) * 3,
        scratch_shapes=scratch,
        compiler_params=pltpu.CompilerParams(
            collective_id=0, has_side_effects=True, vmem_limit_bytes=67043328
        ),
        name="attention_backward",
    )(q, k, v, o, g, lp, ids)
    return pl.pallas_call(
        publish,
        out_shape=shapes,
        in_specs=[any_spec] * 3,
        out_specs=(any_spec,) * 3,
        scratch_shapes=[
            pltpu.VMEM((TOK, HEADS * D), BF16),
            pltpu.VMEM((TOK, GROUPS * D), BF16),
            pltpu.VMEM((TOK, GROUPS * D), BF16),
            dma((3,)),
            dma((3,)),
        ],
        name="publish",
    )(*grads)


def solution(mesh):
    tokens = ("blk", "uly")
    row = P(tokens, None)
    in_specs = (row, row, row, row, row, P(tokens, None, None), P(tokens))
    return jax.shard_map(
        per_device, mesh=mesh, in_specs=in_specs, out_specs=(row, row, row), check_vma=False
    )
```

time: 85.3 us -> 73.3 us (0.86)
  local copies, waits for them, and re-layouts: 8.59 us -> 0 us
  Pallas kernels: 75.7 us -> 72.4 us
    unnamed x17 -> x0, local copies, waits for them, and re-layouts: 8.59 us -> none
    pallas_call x1 -> x2, Pallas kernels: 75.7 us -> 72.4 us  [the longest x1 70.3 us: per_device(): pl.pallas_call(kernel, out_shape=shapes, in_specs=[any_spec] * 5 + [vmem,...]
where the time goes in v2:
time: 73.3 us; the launch traced here: 73 us
  Pallas kernels  72.4 us (99%)
    pallas_call x1, Pallas kernels, per_device(): pl.pallas_call(kernel, out_shape=shapes, in_specs=[any_spec] * 5 + [vmem,...  70.3 us
    pallas_call x1, Pallas kernels, per_device(): pl.pallas_call(publish, out_shape=shapes, in_specs=[any_spec] * 3, out_sp...  2.05 us

profile of v2, /device:TPU:1, one launch (start us, length us, event | category | flops | bytes accessed | tf_op | source)
XLA Modules:
  0.0 73.0 jit_solution(15651647881717909571)
XLA Ops:
  0.6 70.3 %attention_backward.1 = (bf16[128,2048]{1,0:T(8,128)(2,1)}, bf16[128,1024]{1,0:T(8,128)(2,1)}, bf16[128,1024]{1,0:T(8,128)(2,1)}) custom-call(bf16[128,2048]{1,0:T(8,128)(2,1)} %q_in.1, bf16[128,1024]{1,0:T(8,128)(2,1)} %k_in.1, bf16[128,1024]{1,0:T(8,128)(2,1)} %v_in.1, bf16[128,2048]{1,0:T(8,128)(2,1)} %o_in.1, bf16[128,2048]{1,0:T(8,128)(2,1)} %g_in.1, ...), custom_call_target="tpu_custom_call" | custom-call | tf_op jit(solution)/shard_map/attention_backward/pallas_call | solution.py:530
  71.0 2.1 %publish.1 = (bf16[128,2048]{1,0:T(8,128)(2,1)}, bf16[128,1024]{1,0:T(8,128)(2,1)}, bf16[128,1024]{1,0:T(8,128)(2,1)}) custom-call(bf16[128,2048]{1,0:T(8,128)(2,1)} %get-tuple-element.6.q_in, bf16[128,1024]{1,0:T(8,128)(2,1)} %get-tuple-element.7.k_in, bf16[128,1024]{1,0:T(8,128)(2,1)} %get-tuple-element.8.v_in), custom_call_target="tpu_custom_call" | custom-call | tf_op jit(solution)/shard_map/publish/pallas_call | solution.py:541

commit v3 on v2

--- a/solution.py
+++ b/solution.py
@@ -31,10 +31,10 @@
     q_in, k_in, v_in, o_in, g_in, lp_in, id_in,
     q_out, k_out, v_out,
     Q, G, KV, ST, IDT, IDR, IDC,
-    o_s, g_s, q_s, st_src, id_src, SKV, PKV, PQ, PG,
+    o_s, g_s, st_src, id_src, PKV, PQ, PG,
     DQ, ACC0, ACC1, ACC2,
     S2, R2, S1, R1, SO, SQ, XQ, XKV,
-    loc, skv_sem, d2d_send, d2d_recv, yo_send, yo_recv,
+    loc, d2d_send, d2d_recv, yo_send, yo_recv,
     st_send, st_recv, id_send, id_recv,
     hop_send, hop_recv, ret_send, ret_recv,
     oq_send, oq_recv, okv_send, okv_recv, fwd_send, fwd_recv, lout,
@@ -84,13 +84,6 @@
 
     cp_g = pltpu.make_async_copy(g_in, g_s, loc.at[0])
     cp_o = pltpu.make_async_copy(o_in, o_s, loc.at[1])
-    cp_q = pltpu.make_async_copy(q_in, q_s, loc.at[6])
-
-    def stage_kv(g):
-        return (
-            pltpu.make_async_copy(k_in.at[:, narrow(g)], SKV.at[g, :, 0:D], skv_sem.at[0, g]),
-            pltpu.make_async_copy(v_in.at[:, narrow(g)], SKV.at[g, :, D : 2 * D], skv_sem.at[1, g]),
-        )
 
     own = [
         pltpu.make_async_copy(k_in.at[:, narrow(me)], KV.at[0, rows_of(me), 0:D], loc.at[2]),
@@ -109,34 +102,30 @@
     pl.semaphore_signal(barrier, inc=1, device_id=(me, nxt), device_id_type=MESH)
     pl.semaphore_signal(barrier, inc=1, device_id=(me, prv), device_id_type=MESH)
 
-    def stage_step(g, _):
-        for cp in stage_kv(g):
-            cp.start()
-        return 0
-
-    lax.fori_loop(0, GROUPS, stage_step, 0)
     for cp in own:
         cp.start()
-    cp_q.start()
     cp_g.start()
     cp_o.start()
     id_src[...] = jnp.broadcast_to(id_in[...].astype(F32), (8, TOK))
 
-    def stage_wait(g, _):
-        for cp in stage_kv(g):
-            cp.wait()
-        return 0
-
-    lax.fori_loop(0, GROUPS, stage_wait, 0)
     pl.semaphore_wait(barrier, GROUPS + 1)
 
+    def source(kind, g):
+        cols = narrow(g) if kind < 2 else wide(g)
+        return (k_in, v_in, q_in, g_in)[kind].at[:, cols]
+
+    def held(kind, t):
+        return (PKV.at[t, :, 0:D], PKV.at[t, :, D : 2 * D], PQ.at[t], PG.at[t])[kind]
+
+    def final(kind, u):
+        rows = rows_of(u)
+        return (
+            KV.at[0, rows, 0:D], KV.at[0, rows, D : 2 * D], Q.at[rows, :], G.at[rows, :]
+        )[kind]
+
     def mate_copy(kind, t, here, there, same):
-        g = 2 * t + lax.rem(there, 2)
-        src = (SKV.at[g], q_s.at[:, wide(g)], g_s.at[:, wide(g)])[kind]
-        if same:
-            dst = (KV.at[0, rows_of(here), :], Q.at[rows_of(here), :], G.at[rows_of(here), :])[kind]
-        else:
-            dst = (PKV, PQ, PG)[kind].at[t]
+        src = source(kind, 2 * t + lax.rem(there, 2))
+        dst = final(kind, here) if same else held(kind, t)
         return rcopy(src, dst, d2d_send.at[kind, t], d2d_recv.at[kind, t], mate, blk)
 
     def mate_send(kind, k):
@@ -147,6 +136,7 @@
 
     for k in range(NY):
         mate_send(0, k).start()
+        mate_send(1, k).start()
 
     def id_copy(p, src_i):
         return rcopy(id_src, IDT.at[src_i], id_send.at[p], id_recv.at[src_i], p, blk)
@@ -159,13 +149,9 @@
     def y_copy(kind, part, t, s):
         g = 2 * t + core
         u = 2 * s + (core if part == 0 else 1 - core)
-        if part == 0:
-            src = (SKV.at[g], q_s.at[:, wide(g)], g_s.at[:, wide(g)])[kind]
-        else:
-            src = (PKV, PQ, PG)[kind].at[t]
-        dst = (KV.at[0, rows_of(u), :], Q.at[rows_of(u), :], G.at[rows_of(u), :])[kind]
+        src = source(kind, g) if part == 0 else held(kind, t)
         return rcopy(
-            src, dst, yo_send.at[kind, part, t], yo_recv.at[kind, part, s], g, blk
+            src, final(kind, u), yo_send.at[kind, part, t], yo_recv.at[kind, part, s], g, blk
         )
 
     def hop_copy(slot, c):
@@ -182,24 +168,25 @@
 
     for k in range(1, NY):
         y_copy(0, 0, chip(k), y).start()
-    cp_q.wait()
-    cp_g.wait()
-    for kind in (1, 2):
+        y_copy(1, 0, chip(k), y).start()
+    for kind in (2, 3):
         for k in range(NY):
             mate_send(kind, k).start()
+    for k in range(1, NY):
+        for kind in (0, 1):
+            mate_recv(kind, k).wait_recv()
+            y_copy(kind, 1, chip(k), y).start()
     own[0].wait()
     own[1].wait()
     mate_recv(0, 0).wait_recv()
+    mate_recv(1, 0).wait_recv()
     hop_copy(0, chip(0)).start()
-    for k in range(1, NY):
-        mate_recv(0, k).wait_recv()
-        y_copy(0, 1, chip(k), y).start()
     for near in ((1, 2), (3,)):
         for k in near:
-            for kind in (1, 2):
+            for kind in (2, 3):
                 y_copy(kind, 0, chip(k), y).start()
         for k in near:
-            for kind in (1, 2):
+            for kind in (2, 3):
                 mate_recv(kind, k).wait_recv()
                 y_copy(kind, 1, chip(k), y).start()
 
@@ -212,17 +199,17 @@
             tile = jnp.broadcast_to(IDR[slot, s : s + 1, :], (TOK, TOK))
             IDC[slot, s * TOK : (s + 1) * TOK, :] = tile.T
 
-    def wait_kv(k):
-        y_copy(0, 0, y, chip(k)).wait_recv()
-        y_copy(0, 1, y, chip(k)).wait_recv()
-
-    wait_kv(1)
     ids_hop(0).start()
-    hop_copy(0, chip(1)).start()
+    for k in range(1, NY):
+        for kind in (0, 1):
+            for part in (0, 1):
+                y_copy(kind, part, y, chip(k)).wait_recv()
+        hop_copy(0, chip(k)).start()
 
     a, b = lp_in[:, 0, :], lp_in[:, 1, :]
     top = jnp.maximum(a, b)
     lse = (top + jnp.log(jnp.exp(a - top) + jnp.exp(b - top))) * LOG2E
+    cp_g.wait()
     cp_o.wait()
     lane = lax.broadcasted_iota(jnp.int32, (TOK, D), 1)
 
@@ -239,16 +226,11 @@
     ST[me] = st_src[me]
     each_peer(lambda p: st_copy(p, me).start())
 
-    hop_copy(0, chip(0)).wait_recv()
-    hop_copy(1, chip(0)).start()
-    wait_kv(2)
-    hop_copy(0, chip(2)).start()
     ids_hop(0).wait_recv()
     ids_hop(1).start()
-    hop_copy(0, chip(1)).wait_recv()
-    hop_copy(1, chip(1)).start()
-    wait_kv(3)
-    hop_copy(0, chip(3)).start()
+    for k in range(2):
+        hop_copy(0, chip(k)).wait_recv()
+        hop_copy(1, chip(k)).start()
 
     columns_of(0)
     columns_of(1)
@@ -293,26 +275,12 @@
         acc[krows, D : 2 * D] += dv
 
     def wait_qg(k):
-        for kind in (1, 2):
+        for kind in (2, 3):
             y_copy(kind, 0, y, chip(k)).wait_recv()
             y_copy(kind, 1, y, chip(k)).wait_recv()
 
     def own_tiles(qb, count):
         lax.fori_loop(0, count, lambda c, _: (tile(0, c, qb, ACC0, True, QB), 0)[1], 0)
-
-    each_peer(lambda p: st_copy(me, p).wait_recv())
-    own[2].wait()
-    own[3].wait()
-    mate_recv(1, 0).wait_recv()
-    mate_recv(2, 0).wait_recv()
-    wait_qg(1)
-    own_tiles(pair, pair + 1)
-    hop_copy(0, chip(2)).wait_recv()
-    hop_copy(1, chip(2)).start()
-    wait_qg(2)
-    wait_qg(3)
-    ids_hop(1).wait_recv()
-    columns_of(2)
 
     def ret_copy(stage, c):
         rows = chunk(c)
@@ -323,20 +291,65 @@
 
     scales = jnp.where(lax.broadcasted_iota(jnp.int32, (CH, 2 * D), 1) < D, SCALE, 1.0)
 
-    def hop_two(c):
-        hop_copy(1, c).wait_recv()
-        trips = (c * CH) // QB + 1
-        lax.fori_loop(0, trips, lambda qb, _: (tile(2, c, qb, ACC2, False, CH), 0)[1], 0)
+    each_peer(lambda p: st_copy(me, p).wait_recv())
+    own[2].wait()
+    own[3].wait()
+    mate_recv(2, 0).wait_recv()
+    mate_recv(3, 0).wait_recv()
+    wait_qg(1)
+    own_tiles(pair, pair + 1)
+    for k in range(2, NY):
+        hop_copy(0, chip(k)).wait_recv()
+        hop_copy(1, chip(k)).start()
+
+    def two_tiles(c, first, stop):
+        lax.fori_loop(first, stop, lambda qb, _: (tile(2, c, qb, ACC2, False, CH), 0)[1], 0)
+
+    def send_two(c):
         S2[chunk(c), :] = (ACC2[chunk(c), :] * scales).astype(BF16)
         ret_copy(0, c).start()
+
+    ids_hop(1).wait_recv()
+    columns_of(2)
+    hop_copy(1, chip(0)).wait_recv()
+    two_tiles(chip(0), pair, pair + 1)
+
+    @pl.when(pair == 0)
+    def _():
+        send_two(chip(0))
+
+    wait_qg(2)
+    wait_qg(3)
+
+    def hop_one(half):
+        lax.fori_loop(0, ROWS // QB, lambda qb, _: (tile(1, half, qb, ACC1, False, QB), 0)[1], 0)
 
     def pass_on(c):
         ret_copy(0, c).wait_recv()
         S1[chunk(c), :] = (ACC1[chunk(c), :] * scales + R2[chunk(c), :].astype(F32)).astype(BF16)
         ret_copy(1, c).start()
 
-    def hop_one(half):
-        lax.fori_loop(0, ROWS // QB, lambda qb, _: (tile(1, half, qb, ACC1, False, QB), 0)[1], 0)
+    def hop_two(k, _):
+        c = chip(k)
+        late = k // 2
+
+        @pl.when(k > 0)
+        def _():
+            hop_copy(1, c).wait_recv()
+
+        two_tiles(c, 0, pair + (2 - 2 * pair) * late + lax.rem(k, 2) * (1 - late))
+
+        @pl.when(pair + k > 0)
+        def _():
+            send_two(c)
+
+        @pl.when(lax.rem(k, 2) == 1)
+        def _():
+            hop_one(1 - pair + (2 * pair - 1) * late)
+
+        return 0
+
+    lax.fori_loop(0, NCH, hop_two, 0)
 
     def okv_copy(t, s):
         return rcopy(
@@ -357,25 +370,11 @@
         SO[chunk(c), :] = total(c)
         okv_copy(c, y).start()
 
-    def round_trip(j, _):
-        hop_two(chip(j))
-
-        @pl.when(j == 0)
-        def _():
-            hop_copy(0, chip(3)).wait_recv()
-            hop_copy(1, chip(3)).start()
-
-        @pl.when(lax.rem(j, 2) == 1)
-        def _():
-            own_tiles(1 - pair, (2 - pair) * ((3 - j) // 2))
-            hop_one(pair + (1 - 2 * pair) * (j // 2))
-            pass_on(chip(j - 1))
-            pass_on(chip(j))
-
-        return 0
-
-    lax.fori_loop(0, NCH, round_trip, 0)
-    out_chunk(1)
+    pass_on(chip(2))
+    pass_on(chip(3))
+    pass_on(chip(1))
+    pass_on(chip(0))
+    own_tiles(1 - pair, 2 - pair)
 
     mine = pl.ds(mo(core * TOK, TOK), TOK)
     theirs = pl.ds(mo((1 - core) * TOK, TOK), TOK)
@@ -414,13 +413,11 @@
         return 0
 
     lax.fori_loop(1, NY, send_q, 0)
-    XKV[y] = total(y)
-    deliver(y, 1)
-    deliver(y, 2)
     XQ[y] = turn(y)
     deliver(y, 0)
     out_chunk(2)
     out_chunk(3)
+    out_chunk(1)
 
     def arrivals(k, _):
         s = chip(k)
@@ -437,7 +434,11 @@
         deliver(s, 2)
         return 0
 
-    lax.fori_loop(1, NY, arrivals_kv, 0)
+    lax.fori_loop(2, NY, arrivals_kv, 0)
+    XKV[y] = total(y)
+    deliver(y, 1)
+    deliver(y, 2)
+    arrivals_kv(1, 0)
 
     def drain_small(p):
         id_copy(p, me).wait_send()
@@ -451,7 +452,7 @@
             hop_copy(stage, c).wait_send()
             ret_copy(stage, c).wait_send()
     for k in range(NY):
-        for kind in range(3):
+        for kind in range(4):
             mate_send(kind, k).wait_send()
             if k > 0:
                 y_copy(kind, 0, chip(k), y).wait_send()
@@ -472,8 +473,13 @@
 
 def publish(q_in, k_in, v_in, q_out, k_out, v_out, q_s, k_s, v_s, read, write):
     moves = ((q_in, q_s, q_out), (k_in, k_s, k_out), (v_in, v_s, v_out))
-    reads = [pltpu.make_async_copy(a, b, read.at[i]) for i, (a, b, _) in enumerate(moves)]
-    writes = [pltpu.make_async_copy(b, c, write.at[i]) for i, (_, b, c) in enumerate(moves)]
+    reads, writes = [], []
+    for i, (a, b, c) in enumerate(moves):
+        for half in range(2):
+            rows = pl.ds(half * (TOK // 2), TOK // 2)
+            n = 2 * i + half
+            reads.append(pltpu.make_async_copy(a.at[rows, :], b.at[rows, :], read.at[n]))
+            writes.append(pltpu.make_async_copy(b.at[rows, :], c.at[rows, :], write.at[n]))
     for cp in reads:
         cp.start()
     for cp, back in zip(reads, writes):
@@ -502,19 +508,17 @@
         pltpu.VMEM((3, ROWS, TOK), F32),
         pltpu.VMEM((TOK, HEADS * D), BF16),
         pltpu.VMEM((TOK, HEADS * D), BF16),
-        pltpu.VMEM((TOK, HEADS * D), BF16),
         pltpu.VMEM((GROUPS, 8, TOK), F32),
         pltpu.VMEM((8, TOK), F32),
-        pltpu.VMEM((GROUPS, TOK, 2 * D), BF16),
         block, block, block,
         pltpu.VMEM((2 * D, ROWS), F32),
         acc, acc, acc,
         slab, slab, slab, slab, slab, slab,
         pltpu.VMEM((NY, CH, 2 * D), BF16),
         pltpu.VMEM((NY, CH, 2 * D), BF16),
-        dma((7,)), dma((2, GROUPS)),
-        dma((3, NY)), dma((3, NY)),
-        dma((3, 2, NY)), dma((3, 2, NY)),
+        dma((6,)),
+        dma((4, NY)), dma((4, NY)),
+        dma((4, 2, NY)), dma((4, 2, NY)),
         dma((GROUPS,)), dma((GROUPS,)),
         dma((GROUPS,)), dma((GROUPS,)),
         dma((2, NCH + 1)), dma((2, NCH + 1)),
@@ -547,8 +551,8 @@
             pltpu.VMEM((TOK, HEADS * D), BF16),
             pltpu.VMEM((TOK, GROUPS * D), BF16),
             pltpu.VMEM((TOK, GROUPS * D), BF16),
-            dma((3,)),
-            dma((3,)),
+            dma((6,)),
+            dma((6,)),
         ],
         name="publish",
     )(*grads)

time: 73.3 us -> 73.6 us (level)
  no operation moved by 1% of the time
where the time goes in v3:
time: 73.6 us; the launch traced here: 73.5 us
  Pallas kernels  72.8 us (99%)
    pallas_call x1, Pallas kernels, per_device(): pl.pallas_call(kernel, out_shape=shapes, in_specs=[any_spec] * 5 + [vmem,...  70.8 us
    pallas_call x1, Pallas kernels, per_device(): pl.pallas_call(publish, out_shape=shapes, in_specs=[any_spec] * 3, out_sp...  2.01 us

profile of v3, /device:TPU:1, one launch (start us, length us, event | category | flops | bytes accessed | tf_op | source)
XLA Modules:
  0.0 73.5 jit_solution(13686548254508995121)
XLA Ops:
  0.6 70.8 %attention_backward.1 = (bf16[128,2048]{1,0:T(8,128)(2,1)}, bf16[128,1024]{1,0:T(8,128)(2,1)}, bf16[128,1024]{1,0:T(8,128)(2,1)}) custom-call(bf16[128,2048]{1,0:T(8,128)(2,1)} %q_in.1, bf16[128,1024]{1,0:T(8,128)(2,1)} %k_in.1, bf16[128,1024]{1,0:T(8,128)(2,1)} %v_in.1, bf16[128,2048]{1,0:T(8,128)(2,1)} %o_in.1, bf16[128,2048]{1,0:T(8,128)(2,1)} %g_in.1, ...), custom_call_target="tpu_custom_call" | custom-call | tf_op jit(solution)/shard_map/attention_backward/pallas_call | solution.py:534
  71.4 2.0 %publish.1 = (bf16[128,2048]{1,0:T(8,128)(2,1)}, bf16[128,1024]{1,0:T(8,128)(2,1)}, bf16[128,1024]{1,0:T(8,128)(2,1)}) custom-call(bf16[128,2048]{1,0:T(8,128)(2,1)} %get-tuple-element.6.q_in, bf16[128,1024]{1,0:T(8,128)(2,1)} %get-tuple-element.7.k_in, bf16[128,1024]{1,0:T(8,128)(2,1)} %get-tuple-element.8.v_in), custom_call_target="tpu_custom_call" | custom-call | tf_op jit(solution)/shard_map/publish/pallas_call | solution.py:545
